TPU v7x, 32 devices: a whole 2x2x4 slice. The times are simulated.
32 devices in a mesh: wide: 8 (over y, x, core), tp: 4 (over z).
Axes of the slice: x: 2, y: 2, z: 4, core: 2. Of those that a mesh axis runs over, the one named last changes fastest.
Arguments:
- tokens: bfloat16 [16384, 1536], P(('wide', 'tp')), may hold values from -6 to 6
- segment_ids: int32 [16384], P('wide'), may hold values from 0 to 15, never falling along the last dimension, each value on 1 to 2048 neighbouring positions
- out_cotangent: bfloat16 [16384, 1536], P(('wide', 'tp')), may hold values from -6 to 6
- norm_gain: bfloat16 [1536], replicated, may hold values from 0.5 to 1.5
- z_weight: bfloat16 [1536, 3072], P('wide', 'tp'), may hold values from -0.15625 to 0.15625
- x_weight: bfloat16 [1536, 3072], P('wide', 'tp'), may hold values from -0.15625 to 0.15625
- bc_weight: bfloat16 [1536, 256], P('wide', 'tp'), may hold values from -0.15625 to 0.15625
- dt_weight: bfloat16 [1536, 48], P('wide', 'tp'), may hold values from -0.15625 to 0.15625
- x_conv: bfloat16 [4, 3072], replicated, may hold values from -3 to 3
- x_bias: bfloat16 [3072], replicated, may hold values from -3 to 3
- bc_conv: bfloat16 [4, 256], replicated, may hold values from -3 to 3
- bc_bias: bfloat16 [256], replicated, may hold values from -3 to 3
- dt_bias: bfloat16 [48], replicated, may hold values from -6 to -2
- decay_log: bfloat16 [48], replicated, may hold values from -1 to 2
- skip_gain: bfloat16 [48], replicated, may hold values from 0.5 to 1.5
- gate_gain: bfloat16 [3072], replicated, may hold values from 0.5 to 1.5
- out_weight: bfloat16 [3072, 1536], P('tp', 'wide'), may hold values from -0.109375 to 0.109375
Outputs:
- block_out: bfloat16 [16384, 1536], P(('wide', 'tp'))
- grad_x: float32 [16384, 1536], P(('wide', 'tp'))
- norm_gain_grad: float32 [1536], replicated
- z_weight_grad: float32 [1536, 3072], P('wide', 'tp')
- x_weight_grad: float32 [1536, 3072], P('wide', 'tp')
- bc_weight_grad: float32 [1536, 256], P('wide', 'tp')
- dt_weight_grad: float32 [1536, 48], P('wide', 'tp')
- x_conv_grad: float32 [4, 3072], replicated
- x_bias_grad: float32 [3072], replicated
- bc_conv_grad: float32 [4, 256], replicated
- bc_bias_grad: float32 [256], replicated
- dt_bias_grad: float32 [48], replicated
- decay_log_grad: float32 [48], replicated
- skip_gain_grad: float32 [48], replicated
- gate_gain_grad: float32 [3072], replicated
- out_weight_grad: float32 [3072, 1536], P('tp', 'wide')
Inputs may be any that keep to these rules, and one draw needn't show every extreme that they name: `segment_ids`: segment numbers never fall along the stream; each segment holds at most 2048 tokens, and one holds exactly 2048.
All inputs are finite; a program needn't handle non-finite values.
Results may differ from a plain program's by a relative error of at most 0.023.
Values may be sent and summed in bfloat16 or wider, within the bound.
A program may use at most 192 MiB of HBM per device.

v0:
```python
import functools

import jax
import jax.numpy as jnp
from jax import lax
from jax.experimental import pallas as pl
from jax.experimental.pallas import tpu as pltpu
from jax.sharding import PartitionSpec as P


HEADS = 48
HEAD_DIM = 64
STATE = 128
CONV = 4
INNER = 3072
DOC_MAX = 2048
EPS = 1e-05
HALO = 16
Q = 128
LANES = 256
GROUP_HEADS = LANES // HEAD_DIM
F32 = jnp.float32
BF = jnp.bfloat16
HIGH = lax.Precision.HIGHEST
NN = ((1,), (0,))
NT = ((1,), (1,))
TN = ((0,), (0,))
SDS = jax.ShapeDtypeStruct


def mm(a, b, dims=NN, precision=None):
    return lax.dot_general(a, b, (dims, ((), ())), precision=precision, preferred_element_type=F32)


def sigmoid(v):
    return 1.0 / (1.0 + jnp.exp(-v))


def iota(shape, axis):
    return lax.broadcasted_iota(jnp.int32, shape, axis)


def params(vmem_mb=60, **kw):
    return pltpu.CompilerParams(vmem_limit_bytes=vmem_mb * 1024 * 1024, **kw)


def cost(flops, read):
    return pl.CostEstimate(flops=int(flops), bytes_accessed=int(read), transcendentals=0)


def marks_of(ids, halo_ids):
    rows = ids.shape[1]
    here = ids.T
    row, lane = iota(here.shape, 0), iota(here.shape, 1)
    before = [jnp.broadcast_to(halo_ids[0:1, 128 - j : 129 - j], here.shape) for j in range(1, CONV)]
    same = []
    for k in range(1, CONV):
        past = pltpu.roll(here, k, 0)
        for r in range(k):
            past = jnp.where(row == r, before[k - 1 - r], past)
        same.append(past == here)
    firsts, lasts = [], []
    for c in range(rows // Q):
        end = jnp.broadcast_to(here[c * Q + Q - 1 : c * Q + Q, 0:1], (Q, 8))
        start = jnp.broadcast_to(here[c * Q - 1 : c * Q, 0:1], (Q, 8)) if c else before[0][:Q]
        firsts.append(start)
        lasts.append(end)
    first, last = jnp.concatenate(firsts, axis=0), jnp.concatenate(lasts, axis=0)
    marks = same + [None, here == first, here == last, here == before[0], first == last]
    result = here
    for i, mark in enumerate(marks):
        if mark is not None:
            result = jnp.where(lane == i, jnp.where(mark, 1.0, 0.0), result)
    return result


def proj_kernel(tok, halo, gain, ids, halo_ids, weight, x_out, misc_out, normed, turned, info):
    @pl.when(pl.program_id(0) == 0)
    def _():
        for rows, at in ((halo, slice(0, HALO)), (tok, slice(HALO, None))):
            raw = rows[...].astype(F32)
            inv = lax.rsqrt(jnp.mean(raw * raw, axis=-1, keepdims=True) + EPS)
            normed[at] = (raw * inv * gain[...]).astype(BF)
        turned[...] = normed[HALO:].T
        info[...] = marks_of(ids[...], halo_ids[...])

    depth, cols = tok.shape[1], weight.shape[3]
    result = mm(normed[...], weight[...].reshape(depth, cols))
    block = x_out.shape[1]
    x_out[...] = result[:, :block].astype(BF)
    misc_out[0] = result[:, block:].astype(BF)


def project(tokens, halo_rows, gain, ids, halo_ids, weights):
    rows, depth = tokens.shape
    rows = rows + HALO
    nw, nt, k, cols = weights.shape
    block = INNER // nt
    misc = cols - block
    return pl.pallas_call(
        proj_kernel,
        grid=(nt,),
        in_specs=[
            whole_spec(tokens.shape),
            whole_spec(halo_rows.shape),
            whole_spec((1, depth)),
            whole_spec(ids.shape),
            whole_spec(halo_ids.shape),
            pl.BlockSpec((nw, 1, k, cols), lambda t: (0, t, 0, 0)),
        ],
        out_specs=[
            pl.BlockSpec((rows, block), lambda t: (0, t)),
            pl.BlockSpec((1, rows, misc), lambda t: (t, 0, 0)),
            pl.BlockSpec((rows, depth), lambda t: (0, 0)),
            pl.BlockSpec((depth, rows - HALO), lambda t: (0, 0)),
            whole_spec((rows - HALO, 8)),
        ],
        out_shape=[
            SDS((rows, INNER), BF),
            SDS((nt, rows, misc), BF),
            SDS((rows, depth), BF),
            SDS((depth, rows - HALO), BF),
            SDS((rows - HALO, 8), F32),
        ],
        compiler_params=params(),
        cost_estimate=cost(2 * rows * depth * nt * cols, 2 * depth * nt * cols),
        name="project",
    )(tokens, halo_rows, gain, ids, halo_ids, weights)


def plain_kernel(left, weight, out, *turned, first):
    depth, cols = left.shape[1], weight.shape[3]
    if turned:
        @pl.when(pl.program_id(0) == 0)
        def _():
            turned[0][...] = left[...].T

    out[...] = mm(left[first:], weight[...].reshape(depth, cols)).astype(BF)


def plain(left, weights, first, turned):
    rows, depth = left.shape
    rows = rows - first
    nw, nt, k, _ = weights.shape
    block = INNER // nt
    out_specs = [pl.BlockSpec((rows, block), lambda t: (0, t))]
    out_shape = [SDS((rows, INNER), BF)]
    if turned:
        out_specs.append(pl.BlockSpec((depth, rows), lambda t: (0, 0)))
        out_shape.append(SDS((depth, rows), BF))
    return pl.pallas_call(
        functools.partial(plain_kernel, first=first),
        grid=(nt,),
        in_specs=[
            pl.BlockSpec(left.shape, lambda t: (0, 0)),
            pl.BlockSpec((nw, 1, k, block), lambda t: (0, t, 0, 0)),
        ],
        out_specs=out_specs,
        out_shape=out_shape,
        compiler_params=params(),
        cost_estimate=cost(2 * rows * depth * INNER, 2 * depth * INNER),
    )(left, weights)


def select_columns(t, heads, bc_cols, rows, cols):
    lane, col = iota((rows, cols), 0), iota((rows, cols), 1)
    first = (lane < bc_cols) & (col == lane + t * bc_cols)
    second = (
        (lane >= bc_cols)
        & (lane < bc_cols + heads)
        & (col == lane - bc_cols + 2 * STATE + t * heads)
    )
    return jnp.where(first | second, 1.0, 0.0).astype(BF)


def conv_of(ext, taps, bias, info):
    total = bias + taps[0:1] * ext[HALO:]
    for k in range(1, CONV):
        total = total + taps[k : k + 1] * pltpu.roll(ext, k, 0)[HALO:] * info[:, k - 1 : k]
    return total


def head_lanes(group, lanes):
    return jnp.where(
        iota((128, lanes), 0) == group * GROUP_HEADS + iota((128, lanes), 1) // HEAD_DIM, 1.0, 0.0
    ).astype(BF)


def expand(values, selection):
    high = values.astype(BF)
    low = (values - high.astype(F32)).astype(BF)
    return mm(high, selection) + mm(low, selection)


def prepare(misc, info, row_ids, small_rows, bcu, bc, bt, ct, scores, pre, step, rate, cum, cum_t, enter, leave, factor):
    nt, rows_ext, width = misc.shape
    rows = rows_ext - HALO
    chunks = rows // Q
    bc_cols, heads = 2 * STATE // nt, HEADS // nt
    total = None
    for t in range(nt):
        part = mm(misc[t], select_columns(t, heads, bc_cols, width, 2 * STATE + 128))
        total = part if total is None else total + part
    marks = info[...]
    bc_ext = total[:, : 2 * STATE]
    u = conv_of(bc_ext, small_rows[0:CONV], small_rows[CONV : CONV + 1], marks)
    if bcu is not None:
        bcu[...] = bc_ext
    act = (u * sigmoid(u)).astype(BF)
    bc[...] = act
    before = total[HALO:, 2 * STATE :] + small_rows[CONV + 1 : CONV + 2, 0:128]
    steps = jnp.maximum(before, 0.0) + jnp.log1p(jnp.exp(-jnp.abs(before)))
    rates = -jnp.exp(small_rows[CONV + 2 : CONV + 3, 0:128]) * steps
    rates = jnp.where(iota(rates.shape, 1) < HEADS, rates, 0.0)
    if pre is not None:
        pre[...] = before
        rate[...] = rates
    step[...] = steps
    upper = iota((Q, Q), 0) >= iota((Q, Q), 1)
    lower = jnp.where(upper, 1.0, 0.0)
    for c in range(chunks):
        at = slice(c * Q, (c + 1) * Q)
        sums = mm(lower, rates[at], NN, HIGH)
        cum[at] = sums
        cum_t[c] = sums.T
        last = sums[Q - 1 : Q]
        enter[at] = jnp.exp(sums) * marks[at, 4:5]
        leave[at] = jnp.exp(last - sums) * marks[at, 5:6]
        factor[c : c + 1] = jnp.exp(last) * marks[c * Q : c * Q + 1, 7:8]
        bb, cc = act[at, :STATE], act[at, STATE:]
        within = upper & (marks[at, 3:4] == row_ids[0:1, at])
        scores[c] = jnp.where(within, mm(cc, bb, NT), 0.0)
        bt[c] = bb.T
        if ct is not None:
            ct[c] = cc.T


def decay_of(turned, cum_t, c, group, k):
    row = cum_t[c, pl.ds(group * GROUP_HEADS + k, 1), :]
    return jnp.exp(jnp.minimum(turned[:, k : k + 1] - row, 0.0))


def turned_sums(cum, at, group):
    return pltpu.roll(cum[at], (128 - group * GROUP_HEADS) % 128, 1)


def halves(pair):
    left = iota(pair.shape, 1) < HEAD_DIM
    zero = jnp.zeros_like(pair)
    return jnp.concatenate([jnp.where(left, pair, zero), jnp.where(left, zero, pair)], axis=0)


def ssd_kernel(x, misc, info, row_ids, wide_rows, small_rows, signal, y, state, ent, bc_out, bt, scores, step, cum, cum_t, enter, leave, factor):
    group = pl.program_id(0)
    rows = signal.shape[0]
    chunks = rows // Q

    @pl.when(group == 0)
    def _():
        factor[...] = jnp.zeros_like(factor)
        prepare(misc, info, row_ids, small_rows, None, bc_out, bt, None, scores, None, step, None, cum, cum_t, enter, leave, factor)
        base = jnp.zeros((1, 128), F32)
        for c in range(chunks):
            at = slice(c * Q, (c + 1) * Q)
            ent[at] = jnp.exp(cum[at] + base) * info[at, 6:7]
            base = base + cum[c * Q + Q - 1 : c * Q + Q]

    u = conv_of(x[...].astype(F32), wide_rows[0:CONV], wide_rows[CONV : CONV + 1], info[...])
    act = (u * sigmoid(u)).astype(BF)
    signal[...] = act
    pick = head_lanes(group, LANES)
    inputs = act.astype(F32) * expand(step[...], pick)
    inputs_b = inputs.astype(BF)
    weighted = (inputs * expand(leave[...], pick)).astype(BF)
    entering = expand(enter[...], pick)
    factors = expand(factor[...], pick)
    now = jnp.zeros((STATE, LANES), F32)
    whole = jnp.ones((1, LANES), F32)
    for c in range(chunks):
        at = slice(c * Q, (c + 1) * Q)
        turned = turned_sums(cum, at, group)
        pieces = []
        for p in range(LANES // 128):
            ma = (scores[c] * decay_of(turned, cum_t, c, group, 2 * p)).astype(BF)
            mb = (scores[c] * decay_of(turned, cum_t, c, group, 2 * p + 1)).astype(BF)
            pieces.append(mm(jnp.concatenate([ma, mb], axis=1), halves(inputs_b[at, p * 128 : p * 128 + 128])))
        result = jnp.concatenate(pieces, axis=1)
        if c:
            result = result + entering[at] * mm(bc_out[at, STATE:], now.astype(BF))
        y[at] = result.astype(BF)
        now = factors[c : c + 1] * now + mm(bt[c], weighted[at])
        whole = whole * factors[c : c + 1]
    state[0:STATE] = now.astype(BF)
    state[STATE:] = jnp.broadcast_to(whole, (16, LANES)).astype(BF)


def whole_spec(shape):
    return pl.BlockSpec(shape, lambda *_: (0,) * len(shape))


def column_spec(rows):
    return pl.BlockSpec((rows, LANES), lambda g: (0, g))


def ssd_forward(x_ext, misc, info, row_ids, wide_rows, small_rows):
    rows = x_ext.shape[0] - HALO
    chunks = rows // Q
    return pl.pallas_call(
        ssd_kernel,
        grid=(INNER // LANES,),
        in_specs=[
            column_spec(rows + HALO),
            whole_spec(misc.shape),
            whole_spec(info.shape),
            whole_spec(row_ids.shape),
            column_spec(8),
            whole_spec(small_rows.shape),
        ],
        out_specs=[
            column_spec(rows),
            column_spec(rows),
            column_spec(STATE + 16),
            whole_spec((rows, 128)),
            whole_spec((rows, 2 * STATE)),
        ],
        out_shape=[
            SDS((rows, INNER), BF),
            SDS((rows, INNER), BF),
            SDS((STATE + 16, INNER), BF),
            SDS((rows, 128), F32),
            SDS((rows, 2 * STATE), BF),
        ],
        scratch_shapes=[
            pltpu.VMEM((chunks, STATE, Q), BF),
            pltpu.VMEM((chunks, Q, Q), F32),
            pltpu.VMEM((rows, 128), F32),
            pltpu.VMEM((rows, 128), F32),
            pltpu.VMEM((chunks, 128, Q), F32),
            pltpu.VMEM((rows, 128), F32),
            pltpu.VMEM((rows, 128), F32),
            pltpu.VMEM((8, 128), F32),
        ],
        compiler_params=params(),
        cost_estimate=cost(20e9, 12e6),
        name="ssd_forward",
    )(x_ext, misc, info, row_ids, wide_rows, small_rows)


GATE_LANES = 1024


def gate_kernel(y, signal, gate, dno, bc, ent, incoming, wide_rows, pair, d_y, adjoint, sums, y_sum, gated_sum, acc):
    block = pl.program_id(0)
    rows = y.shape[0]
    width = GATE_LANES
    pieces = INNER // width

    @pl.when(block == 0)
    def _():
        acc[...] = jnp.zeros_like(acc)
        sums[...] = jnp.zeros_like(sums)

    cc = bc[:, STATE:]
    cc_t = cc.T
    ent_hi = ent[...].astype(BF)
    ent_lo = (ent[...] - ent_hi.astype(F32)).astype(BF)

    def lanes_of(i):
        pick = jnp.where(
            iota((128, width), 0) == i * (width // HEAD_DIM) + iota((128, width), 1) // HEAD_DIM, 1.0, 0.0
        ).astype(BF)
        return mm(ent_hi, pick) + mm(ent_lo, pick)

    def first(i, carry):
        squares, dots = carry
        at = pl.ds(pl.multiple_of(i * width, width), width)
        total = y[:, at].astype(F32) + wide_rows[CONV + 1 : CONV + 2, at] * signal[:, at].astype(F32)
        total = total + lanes_of(i) * mm(cc, incoming[0:STATE, at])
        z = gate[:, at].astype(F32)
        gated = total * (z * sigmoid(z))
        y_sum[:, at] = total
        gated_sum[:, at] = gated
        squares = squares + jnp.sum(gated * gated, axis=-1, keepdims=True)
        dots = dots + jnp.sum(dno[:, at].astype(F32) * wide_rows[CONV + 2 : CONV + 3, at] * gated, axis=-1, keepdims=True)
        return squares, dots

    zero = jnp.zeros((rows, 1), F32)
    squares, dots = lax.fori_loop(0, pieces, first, (zero, zero))
    inv = lax.rsqrt(squares / INNER + EPS)
    pull = inv * inv * inv * (dots / INNER)

    def second(i, carry):
        at = pl.ds(pl.multiple_of(i * width, width), width)
        total, gated = y_sum[:, at], gated_sum[:, at]
        z = gate[:, at].astype(F32)
        logistic = sigmoid(z)
        d_out = dno[:, at].astype(F32)
        scaled = gated * inv
        pair[1, :, at] = (scaled * wide_rows[CONV + 2 : CONV + 3, at]).astype(BF)
        d_gated = inv * (d_out * wide_rows[CONV + 2 : CONV + 3, at]) - gated * pull
        dy = d_gated * (z * logistic)
        d_y[:, at] = dy.astype(BF)
        pair[0, :, at] = (d_gated * total * logistic * (1.0 + z * (1.0 - logistic))).astype(BF)
        acc[:, at] += mm(cc_t, (dy * lanes_of(i)).astype(BF))
        sums[0:1, at] += jnp.sum(d_out * scaled, axis=0, keepdims=True)
        sums[1:2, at] += jnp.sum(dy * signal[:, at].astype(F32), axis=0, keepdims=True)
        return carry

    lax.fori_loop(0, pieces, second, 0)

    @pl.when(block == pl.num_programs(0) - 1)
    def _():
        adjoint[...] = acc[...].astype(BF)


def gate_norm(y, signal, gate, dno, bc, ent, incoming, wide_rows):
    rows = y.shape[0]
    size = min(rows, 256)
    row = lambda cols: pl.BlockSpec((size, cols), lambda i: (i, 0))
    return pl.pallas_call(
        gate_kernel,
        grid=(rows // size,),
        in_specs=[
            row(INNER), row(INNER), row(INNER), row(INNER), row(2 * STATE), row(128),
            whole_spec(incoming.shape), whole_spec(wide_rows.shape),
        ],
        out_specs=[
            pl.BlockSpec((2, size, INNER), lambda i: (0, i, 0)), row(INNER), whole_spec((STATE, INNER)), whole_spec((8, INNER)),
        ],
        out_shape=[
            SDS((2, rows, INNER), BF), SDS((rows, INNER), BF), SDS((STATE, INNER), BF), SDS((8, INNER), F32),
        ],
        scratch_shapes=[
            pltpu.VMEM((size, INNER), F32), pltpu.VMEM((size, INNER), F32), pltpu.VMEM((STATE, INNER), F32),
        ],
        compiler_params=params(),
        cost_estimate=cost(10e9, 25e6),
        name="gate_norm",
    )(y, signal, gate, dno, bc, ent, incoming, wide_rows)


def conv_back(du, ext, taps, info):
    grads = []
    zero = jnp.zeros((HALO, du.shape[1]), F32)
    back = None
    for k in range(CONV):
        part = du if k == 0 else du * info[:, k - 1 : k]
        moved = ext if k == 0 else pltpu.roll(ext, k, 0)
        grads.append(jnp.sum(part * moved[HALO:], axis=0, keepdims=True))
        term = jnp.concatenate([zero, part * taps[k : k + 1]], axis=0)
        if k:
            term = pltpu.roll(term, term.shape[0] - k, 0)
        back = term if back is None else back + term
    grads.append(jnp.sum(du, axis=0, keepdims=True))
    grads.append(jnp.zeros((3, du.shape[1]), F32))
    return back, jnp.concatenate(grads, axis=0)


def slope_of(u):
    logistic = sigmoid(u)
    return logistic * (1.0 + u * (1.0 - logistic))


def ssd_back_kernel(
    x, signal, dy, misc, info, row_ids, wide_rows, small_rows, incoming, after,
    dx, tail, rim, conv_grad, small, tail_bc, rim_bc, bc_grad, head_grad,
    bcu, bc, bt, ct, scores, pre, step, rate, cum, cum_t, enter, leave, factor,
    d_scores, d_b, d_c, d_direct, d_enter, d_leave, d_rows, d_cols, d_factor,
):
    group = pl.program_id(0)
    rows = signal.shape[0]
    chunks = rows // Q

    @pl.when(group == 0)
    def _():
        factor[...] = jnp.zeros_like(factor)
        prepare(misc, info, row_ids, small_rows, bcu, bc, bt, ct, scores, pre, step, rate, cum, cum_t, enter, leave, factor)
        for ref in (d_scores, d_b, d_c, d_direct, d_enter, d_leave, d_rows, d_cols, d_factor):
            ref[...] = jnp.zeros_like(ref)

    pick = head_lanes(group, LANES)
    gather = jnp.where(
        iota((LANES, 128), 1) == group * GROUP_HEADS + iota((LANES, 128), 0) // HEAD_DIM, 1.0, 0.0
    ).astype(BF)
    act = signal[...].astype(F32)
    steps = expand(step[...], pick)
    inputs = act * steps
    inputs_b = inputs.astype(BF)
    leaving = expand(leave[...], pick)
    weighted = inputs * leaving
    weighted_b = weighted.astype(BF)
    cot = dy[...].astype(F32)
    cot_in = cot * expand(enter[...], pick)
    cot_in_b = cot_in.astype(BF)
    factors = expand(factor[...], pick)
    now = incoming[0:STATE].astype(F32)
    states = []
    for c in range(chunks):
        at = slice(c * Q, (c + 1) * Q)
        states.append(now.astype(BF))
        if c < chunks - 1:
            now = factors[c : c + 1] * now + mm(bt[c], weighted_b[at])
    adj = after[0:STATE].astype(F32)
    lane = iota((Q, 128), 1)
    d_signal = [None] * chunks
    for c in reversed(range(chunks)):
        at = slice(c * Q, (c + 1) * Q)
        bb, cc = bc[at, :STATE], bc[at, STATE:]
        adj_b = adj.astype(BF)
        from_state = mm(cc, states[c])
        from_adj = mm(bb, adj_b)
        d_c[at] += mm(cot_in_b[at], states[c], NT)
        d_b[at] += mm(weighted_b[at], adj_b, NT)
        crossing = factors[c : c + 1] * jnp.sum(adj * states[c].astype(F32), axis=0, keepdims=True)
        d_factor[c] += mm(jnp.broadcast_to(crossing, (8, LANES)).astype(BF), gather)
        turned = turned_sums(cum, at, group)
        masked = scores[c]
        pieces = []
        score_sum = None
        row_sum = jnp.zeros((Q, 128), F32)
        for p in range(LANES // 128):
            lanes = slice(p * 128, p * 128 + 128)
            cots = halves(dy[at, lanes])
            d_pair = mm(cots, inputs_b[at, lanes], NT)
            both = []
            for j in range(2):
                k = 2 * p + j
                decays = decay_of(turned, cum_t, c, group, k)
                both.append((masked * decays).astype(BF))
                through = d_pair[j * Q : (j + 1) * Q] * decays
                score_sum = through if score_sum is None else score_sum + through
                product = through * masked
                row_sum = jnp.where(
                    lane == group * GROUP_HEADS + k, jnp.sum(product, axis=1, keepdims=True), row_sum
                )
                d_cols[c, pl.ds(group * GROUP_HEADS + k, 1), :] = jnp.sum(product, axis=0, keepdims=True)
            pieces.append(mm(jnp.concatenate(both, axis=0), cots, TN))
        d_scores[c] += score_sum
        d_rows[at] += row_sum
        d_inputs = jnp.concatenate(pieces, axis=1) + leaving[at] * from_adj
        d_direct[at] += mm((act[at] * d_inputs).astype(BF), gather)
        d_enter[at] += mm((cot_in[at] * from_state).astype(BF), gather)
        d_leave[at] += mm((weighted[at] * from_adj).astype(BF), gather)
        d_signal[c] = steps[at] * d_inputs + wide_rows[CONV + 1 : CONV + 2] * cot[at]
        if c:
            adj = factors[c : c + 1] * adj + mm(ct[c], cot_in_b[at])
    ext = x[...].astype(F32)
    du = jnp.concatenate(d_signal, axis=0) * slope_of(conv_of(ext, wide_rows[0:CONV], wide_rows[CONV : CONV + 1], info[...]))
    back, grads = conv_back(du, ext, wide_rows[0:CONV], info[...])
    dx[...] = back[HALO:].astype(BF)
    tail[...] = back[rows + HALO - 8 :]
    rim[...] = back[HALO - 8 : HALO]
    conv_grad[...] = grads

    @pl.when(group == pl.num_programs(0) - 1)
    def _():
        after_eq = jnp.where(iota((Q, Q), 1) >= iota((Q, Q), 0), 1.0, 0.0)
        before_ne = jnp.where(iota((Q, Q), 1) < iota((Q, Q), 0), 1.0, 0.0)
        grow = -jnp.exp(small_rows[CONV + 2 : CONV + 3, 0:128])
        dec_sum = jnp.zeros((1, 128), F32)
        bias_sum = jnp.zeros((1, 128), F32)
        valid = iota((Q, 128), 1) < HEADS
        parts = []
        for c in range(chunks):
            at = slice(c * Q, (c + 1) * Q)
            bb, cc = bc[at, :STATE], bc[at, STATE:]
            within = (iota((Q, Q), 0) >= iota((Q, Q), 1)) & (info[at, 3:4] == row_ids[0:1, at])
            ds = jnp.where(within, d_scores[c], 0.0).astype(BF)
            parts.append(jnp.concatenate([d_b[at] + mm(ds, cc, TN), d_c[at] + mm(ds, bb)], axis=1))
            d_rate = mm(after_eq, d_rows[at] + d_enter[at] - d_cols[c].T, NN, HIGH)
            d_rate = d_rate + mm(before_ne, d_leave[at], NN, HIGH) + d_factor[c][0:1]
            d_step = d_direct[at] + grow * d_rate
            d_pre = jnp.where(valid, d_step * sigmoid(pre[at]), 0.0)
            small[at, 2 * STATE :] = d_pre.astype(BF)
            bias_sum = bias_sum + jnp.sum(d_pre, axis=0, keepdims=True)
            dec_sum = dec_sum + jnp.sum(jnp.where(valid, d_rate * rate[at], 0.0), axis=0, keepdims=True)
        ext_bc = bcu[...]
        du_bc = jnp.concatenate(parts, axis=0)
        du_bc = du_bc * slope_of(conv_of(ext_bc, small_rows[0:CONV], small_rows[CONV : CONV + 1], info[...]))
        back_bc, grads_bc = conv_back(du_bc, ext_bc, small_rows[0:CONV], info[...])
        small[:, : 2 * STATE] = back_bc[HALO:].astype(BF)
        tail_bc[...] = back_bc[rows + HALO - 8 :]
        rim_bc[...] = back_bc[HALO - 8 : HALO]
        bc_grad[...] = grads_bc
        head_grad[...] = jnp.concatenate([bias_sum, dec_sum, jnp.zeros((6, 128), F32)], axis=0)


def ssd_backward(x_ext, signal, dy, misc, info, row_ids, wide_rows, small_rows, incoming, after):
    rows = signal.shape[0]
    chunks = rows // Q
    vm = pltpu.VMEM
    return pl.pallas_call(
        ssd_back_kernel,
        grid=(INNER // LANES,),
        in_specs=[
            column_spec(rows + HALO),
            column_spec(rows),
            column_spec(rows),
            whole_spec(misc.shape),
            whole_spec(info.shape),
            whole_spec(row_ids.shape),
            column_spec(8),
            whole_spec(small_rows.shape),
            column_spec(incoming.shape[0]),
            column_spec(after.shape[0]),
        ],
        out_specs=[
            column_spec(rows),
            column_spec(8),
            column_spec(8),
            column_spec(8),
            whole_spec((rows, 2 * STATE + 128)),
            whole_spec((8, 2 * STATE)),
            whole_spec((8, 2 * STATE)),
            whole_spec((8, 2 * STATE)),
            whole_spec((8, 128)),
        ],
        out_shape=[
            SDS((rows, INNER), BF),
            SDS((8, INNER), F32),
            SDS((8, INNER), F32),
            SDS((8, INNER), F32),
            SDS((rows, 2 * STATE + 128), BF),
            SDS((8, 2 * STATE), F32),
            SDS((8, 2 * STATE), F32),
            SDS((8, 2 * STATE), F32),
            SDS((8, 128), F32),
        ],
        scratch_shapes=[
            vm((rows + HALO, 2 * STATE), F32),
            vm((rows, 2 * STATE), BF),
            vm((chunks, STATE, Q), BF),
            vm((chunks, STATE, Q), BF),
            vm((chunks, Q, Q), F32),
            vm((rows, 128), F32),
            vm((rows, 128), F32),
            vm((rows, 128), F32),
            vm((rows, 128), F32),
            vm((chunks, 128, Q), F32),
            vm((rows, 128), F32),
            vm((rows, 128), F32),
            vm((8, 128), F32),
            vm((chunks, Q, Q), F32),
            vm((rows, 128), F32),
            vm((rows, 128), F32),
            vm((rows, 128), F32),
            vm((rows, 128), F32),
            vm((rows, 128), F32),
            vm((rows, 128), F32),
            vm((chunks, 128, Q), F32),
            vm((chunks, 8, 128), F32),
        ],
        compiler_params=params(),
        cost_estimate=cost(40e9, 15e6),
        name="ssd_backward",
    )(x_ext, signal, dy, misc, info, row_ids, wide_rows, small_rows, incoming, after)


def slot_of(piece, order):
    slot = 0
    for j, bit in enumerate(order[1:], 2):
        slot = slot + (((piece >> bit) & 1) << (len(order) - j))
    return slot


def weight_grad_body(where, own_z, next_z, own_o, next_o, own, other, *outs, cols, top):
    kind, piece = pl.program_id(0), pl.program_id(1)
    keep_a, send_a, keep_b, send_b = outs
    half = keep_a.shape[3]
    per = half // cols
    nt = 2 * per
    block = INNER // nt
    mine = jnp.where(kind == 0, own_z[0], own_o[0])
    theirs = jnp.where(kind == 0, next_z[0], next_o[0])
    parts = []
    for turn in range(nt):
        t = jnp.bitwise_xor(where[1], turn)
        at = pl.ds(pl.multiple_of(t * block, block), block)
        parts.append((mm(mine, own[0, :, at]) + mm(theirs, other[0, :, at])).astype(BF))
    for keep, send, order, chosen in (
        (keep_a, send_a, list(range(top + 1)), parts[:per]),
        (keep_b, send_b, list(range(top, -1, -1)), parts[per:]),
    ):
        slot = slot_of(piece, order)
        away = (piece >> order[0]) & 1

        @pl.when(away == 0)
        def _(keep=keep, slot=slot, chosen=chosen):
            for i, value in enumerate(chosen):
                keep[0, slot, :, i * cols : (i + 1) * cols] = value

        @pl.when(away == 1)
        def _(send=send, slot=slot, chosen=chosen):
            for i, value in enumerate(chosen):
                send[0, slot, :, i * cols : (i + 1) * cols] = value


def weight_grad(where, lefts, own, other, nt, cols):
    nw, k, rows = lefts[0].shape
    nm = nw // 2
    half = nt // 2 * cols
    left = pl.BlockSpec((1, k, rows), lambda q, r, s: (2 * jnp.bitwise_xor(r, s[0]) + s[2], 0, 0))
    right = pl.BlockSpec((1, rows, INNER), lambda q, r, s: (q, 0, 0))
    out = pl.BlockSpec((1, nm // 2, k, half), lambda q, r, s: (q, 0, 0, 0))
    return pl.pallas_call(
        functools.partial(weight_grad_body, cols=cols, top=nm.bit_length() - 2),
        grid_spec=pltpu.PrefetchScalarGridSpec(
            num_scalar_prefetch=1,
            grid=(2, nm),
            in_specs=[left] * 4 + [right] * 2,
            out_specs=[out] * 4,
        ),
        out_shape=[SDS((2, nm // 2, k, half), BF)] * 4,
        compiler_params=params(),
        cost_estimate=cost(8 * nm * k * rows * INNER, 12 * nm * k * INNER),
    )(where, *lefts, own, other)


def out_kernel(left, weight, tokens, out, acc):
    t = pl.program_id(0)
    depth = out.shape[1]
    part = mm(left[0], weight[...].reshape(depth, weight.shape[3]), NT)

    @pl.when(t == 0)
    def _():
        acc[...] = tokens[...].astype(F32) + part

    @pl.when(t > 0)
    def _():
        acc[...] += part

    @pl.when(t == pl.num_programs(0) - 1)
    def _():
        out[...] = acc[...].astype(BF)


def out_project(left, weights, which, tokens):
    rows, depth = tokens.shape
    nw, nt, k, _ = weights.shape
    block = INNER // nt
    return pl.pallas_call(
        out_kernel,
        grid=(nt,),
        in_specs=[
            pl.BlockSpec((1, rows, block), lambda t: (1, 0, t)),
            pl.BlockSpec((nw, 1, k, block), lambda t: (0, t, 0, which)),
            whole_spec(tokens.shape),
        ],
        out_specs=whole_spec(tokens.shape),
        out_shape=SDS(tokens.shape, BF),
        scratch_shapes=[pltpu.VMEM((rows, depth), F32)],
        compiler_params=params(),
        cost_estimate=cost(2 * rows * depth * INNER, 2 * depth * INNER),
        name="out_project",
    )(left, weights, tokens)


def gate_part_kernel(left, weight, out):
    t = pl.program_id(0)
    depth = out.shape[1]
    part = mm(left[0], weight[...].reshape(depth, weight.shape[3]), NT)

    @pl.when(t == 0)
    def _():
        out[...] = part

    @pl.when(t > 0)
    def _():
        out[...] += part


def gate_part(left, weights, which, depth):
    rows = left.shape[1]
    nw, nt, k, _ = weights.shape
    block = INNER // nt
    return pl.pallas_call(
        gate_part_kernel,
        grid=(nt,),
        in_specs=[
            pl.BlockSpec((1, rows, block), lambda t: (0, 0, t)),
            pl.BlockSpec((nw, 1, k, block), lambda t: (0, t, 0, which)),
        ],
        out_specs=whole_spec((rows, depth)),
        out_shape=SDS((rows, depth), F32),
        compiler_params=params(),
        cost_estimate=cost(2 * rows * depth * INNER, 2 * depth * INNER),
        name="gate_part",
    )(left, weights)


MESH = pl.DeviceIdType.MESH
SPLIT = 4
RATE = 2
LAG = 2


def remote(src, dst, send, recv, peer):
    return pltpu.make_async_remote_copy(src, dst, send, recv, device_id=peer, device_id_type=MESH)


def greet(peers):
    barrier = pltpu.get_barrier_semaphore()
    for peer in peers:
        pl.semaphore_signal(barrier, inc=1, device_id=peer, device_id_type=MESH)
    pl.semaphore_wait(barrier, len(peers))


class Line:
    def __init__(self, own, slot, send, recv, count):
        self.own, self.slot, self.send, self.recv, self.count = own, slot, send, recv, count
        self.t = lax.axis_index("tp")

    def each(self, distance, leaving, act):
        t, last = self.t, self.count - 1
        for way, sign in ((0, 1), (1, -1)):
            origin = t - sign * distance
            ahead = t + sign
            fine = (origin >= 0) & (origin <= last)
            if leaving:
                fine = fine & (ahead >= 0) & (ahead <= last)
            step = distance + 1 if leaving else distance

            @pl.when(fine)
            def _(origin=origin, ahead=ahead, way=way, step=step):
                there = self.slot(jnp.clip(origin, 0, last))
                source = self.own if leaving and distance == 0 else there
                act(
                    remote(source, there, self.send.at[way, step], self.recv.at[way, step], {"tp": jnp.clip(ahead, 0, last)})
                )

    def start(self, distance):
        self.each(distance, True, lambda copy: copy.start())

    def arrive(self, distance):
        self.each(distance, False, lambda copy: copy.wait_recv())

    def finish(self):
        for distance in range(self.count - 1):
            self.each(distance, True, lambda copy: copy.wait_send())


def gather_kernel(own, z_own, o_own, whole, z_line, o_line, send_x, recv_x, send_z, recv_z, send_o, recv_o, send_p, recv_p, send_c, recv_c, local):
    nw, nt = whole.shape[0], whole.shape[1]
    k = own.shape[0]
    w, t = lax.axis_index("wide"), lax.axis_index("tp")
    bits = nw.bit_length() - 2
    rows = k // SPLIT
    half = nt // 2
    greet(
        [{"tp": lax.rem(t + 1, nt)}, {"tp": lax.rem(t + nt - 1, nt)}]
        + [{"wide": jnp.bitwise_xor(w, 1 << b)} for b in range(bits + 1)]
    )
    part = lambda s: pl.ds(s * rows, rows)
    mine = []
    for s in range(SPLIT):
        mine.append(pltpu.make_async_copy(own.at[part(s)], whole.at[w, t, part(s)], local.at[0, s]))
        mine.append(pltpu.make_async_copy(z_own.at[part(s)], z_line.at[t, part(s)], local.at[1, s]))
        mine.append(pltpu.make_async_copy(o_own.at[part(s)], o_line.at[t, part(s)], local.at[2, s]))
    first = [Line(own.at[part(s)], lambda o, s=s: whole.at[w, o, part(s)], send_x.at[s], recv_x.at[s], nt) for s in range(SPLIT)]
    later = [Line(z_own.at[part(s)], lambda o, s=s: z_line.at[o, part(s)], send_z.at[s], recv_z.at[s], nt) for s in range(SPLIT)]
    later += [Line(o_own.at[part(s)], lambda o, s=s: o_line.at[o, part(s)], send_o.at[s], recv_o.at[s], nt) for s in range(SPLIT)]
    for line in first:
        line.start(0)
    for copy in mine:
        copy.start()
    sent, crossing, have, coming = [], [], {}, {}

    def exchange(index, h, s, mask, send, recv):
        at = (pl.ds(h * half, half), part(s))
        peer = {"wide": jnp.bitwise_xor(w, mask)}
        ref = whole.at[(index,) + at]
        copy = remote(ref, ref, send, recv, peer)
        copy.start()
        sent.append(copy)
        other = whole.at[(jnp.bitwise_xor(index, mask),) + at]
        return remote(other, other, send, recv, peer)

    def cross(index, h, s, number):
        crossing.append(exchange(index, h, s, 1, send_c.at[s, h, number], recv_c.at[s, h, number]))

    def begin(s, p):
        for h in range(2):
            mask = 2 << (p if h == 0 else bits - 1 - p)
            coming[s, p, h] = []
            for n, index in enumerate(list(have[s, h])):
                slot = (1 << p) - 1 + n
                copy = exchange(index, h, s, mask, send_p.at[s, h, slot], recv_p.at[s, h, slot])
                coming[s, p, h].append((jnp.bitwise_xor(index, mask), copy))

    hops = nt - 1
    pending = len(later)
    for tick in range(max(SPLIT + hops - 1 + bits, (pending + RATE - 1) // RATE + hops + LAG)):
        for d in range(hops, 0, -1):
            s = tick - d + 1
            if 0 <= s < SPLIT:
                first[s].arrive(d)
                if d < hops:
                    first[s].start(d)
        s = tick - hops + 1
        if 0 <= s < SPLIT:
            mine[3 * s].wait()
            for h in range(2):
                have[s, h] = [w]
            begin(s, 0)
            for h in range(2):
                cross(w, h, s, 0)
        for p in range(bits):
            s = tick - hops - p
            if 0 <= s < SPLIT:
                for h in range(2):
                    for index, copy in coming[s, p, h]:
                        copy.wait_recv()
                        have[s, h].append(index)
                if p + 1 < bits:
                    begin(s, p + 1)
                for h in range(2):
                    for n in range(1 << p):
                        cross(coming[s, p, h][n][0], h, s, (1 << p) + n)
        for d in range(hops, -1, -1):
            for n in range(RATE * (tick - LAG - d), RATE * (tick - LAG - d + 1)):
                if 0 <= n < pending:
                    if d:
                        later[n].arrive(d)
                    if d < hops:
                        later[n].start(d)
    for copy in crossing:
        copy.wait_recv()
    for s in range(SPLIT):
        mine[3 * s + 1].wait()
        mine[3 * s + 2].wait()
    for line in first + later:
        line.finish()
    for copy in sent:
        copy.wait_send()


def gather(own, z_own, o_own, nw, nt):
    k, cols = own.shape
    nm = nw // 2
    dma = pltpu.SemaphoreType.DMA
    return pl.pallas_call(
        gather_kernel,
        in_specs=[pl.BlockSpec(memory_space=pltpu.VMEM)] * 3,
        out_specs=[pl.BlockSpec(memory_space=pl.ANY)] * 3,
        out_shape=[SDS((nw, nt, k, cols), BF), SDS((nt,) + z_own.shape, BF), SDS((nt,) + o_own.shape, BF)],
        scratch_shapes=[dma((SPLIT, 2, nt))] * 6 + [dma((SPLIT, 2, nm))] * 4 + [dma((3, SPLIT))],
        compiler_params=params(32, collective_id=0, has_side_effects=True),
        cost_estimate=cost(60e9, 1e6),
        name="gather",
    )(own, z_own, o_own)


def span_shifts(span):
    reach = (DOC_MAX - 2) // span + 1
    size, steps = 1, []
    while 2 * size < reach:
        steps.append(size)
        size *= 2
    return steps, (1 + size if size < reach else 0)


STATE_PARTS = 4
EARLY = 1


def join(near, far):
    decay = near[STATE : STATE + 1].astype(F32)
    state = near[:STATE].astype(F32) + decay * far[:STATE].astype(F32)
    whole = near[STATE:].astype(F32) * far[STATE:].astype(F32)
    return jnp.concatenate([state, whole], axis=0).astype(BF)


class Passing:
    def __init__(self, source, target, send, recv, steps):
        nt = lax.axis_size("tp")
        count = lax.axis_size("wide") * nt
        place = lax.axis_index("wide") * nt + lax.axis_index("tp")
        ahead = place + steps
        behind = place - steps
        self.sends = (ahead < count) & (ahead >= 0)
        self.gets = (behind < count) & (behind >= 0)
        to = jnp.clip(ahead, 0, count - 1)
        self.peer = {"wide": to // nt, "tp": lax.rem(to, nt)}
        self.source, self.target, self.send, self.recv = source, target, send, recv

    def copy(self, j):
        width = INNER // STATE_PARTS
        at = pl.ds(j * width, width)
        return remote(self.source.at[:, at], self.target.at[:, at], self.send.at[j], self.recv.at[j], self.peer)

    def clear(self):
        @pl.when(jnp.logical_not(self.gets))
        def _():
            self.target[...] = jnp.zeros_like(self.target)

    def start(self, j):
        @pl.when(self.sends)
        def _():
            self.copy(j).start()

    def arrive(self, j):
        @pl.when(self.gets)
        def _():
            self.copy(j).wait_recv()

    def finish(self):
        @pl.when(self.sends)
        def _():
            for j in range(STATE_PARTS):
                self.copy(j).wait_send()


def shift_peers(shifts):
    nt = lax.axis_size("tp")
    count = lax.axis_size("wide") * nt
    place = lax.axis_index("wide") * nt + lax.axis_index("tp")
    peers = []
    for steps in shifts:
        for sign in (1, -1):
            to = lax.rem(place + count + sign * steps, count)
            peers.append({"wide": to // nt, "tp": lax.rem(to, nt)})
    return peers


def spread_kernel(state, z_line, z_first, o_line, o_first, incoming, z_whole, o_whole, *scratch, span):
    steps, far_step = span_shifts(span)
    levels = len(steps) + 1 + (1 if far_step else 0)
    buffers, scratch = scratch[:levels], scratch[levels:]
    helds, scratch = scratch[: len(steps)], scratch[len(steps) :]
    send_s, recv_s, send_p, recv_p, send_c, recv_c, local = scratch
    nw, nt = z_whole.shape[0], z_whole.shape[1]
    w = lax.axis_index("wide")
    bits = nw.bit_length() - 2
    shifts = sorted(set(steps) | {1} | ({far_step} if far_step else set()))
    width = INNER // STATE_PARTS

    def columns(j):
        return slice(j * width, (j + 1) * width)

    sources = [state] + list(helds)
    passes = [Passing(sources[i], buffers[i], send_s.at[i], recv_s.at[i], steps[i]) for i in range(len(steps))]
    last = sources[len(steps)]
    near = Passing(last, buffers[len(steps)], send_s.at[len(steps)], recv_s.at[len(steps)], 1)
    ends = [near]
    if far_step:
        ends.append(Passing(last, buffers[len(steps) + 1], send_s.at[len(steps) + 1], recv_s.at[len(steps) + 1], far_step))
    for item in passes + ends:
        item.clear()
    greet(shift_peers(shifts) + [{"wide": jnp.bitwise_xor(w, 1 << b)} for b in range(bits + 1)])
    for j in range(STATE_PARTS):
        (passes + ends)[0].start(j)
    if not passes and far_step:
        for j in range(STATE_PARTS):
            ends[1].start(j)

    sent, copies, crossing = [], [], []
    kinds = ((z_line, z_first, z_whole, [2 << p for p in range(bits)]), (o_line, o_first, o_whole, [2 << (bits - 1 - p) for p in range(bits)]))

    def exchange(source, whole, index, c, mask, send, recv):
        peer = {"wide": jnp.bitwise_xor(w, mask)}
        copy = remote(source, whole.at[index, c], send, recv, peer)
        copy.start()
        sent.append(copy)
        other = whole.at[jnp.bitwise_xor(index, mask), c]
        return remote(other, other, send, recv, peer)

    waiting = {}
    for kind, (line, first, whole, masks) in enumerate(kinds):
        waiting[kind] = {c: [(w, line.at[c]), (jnp.bitwise_xor(w, masks[0]), first.at[c])] for c in range(nt)}
    rounds = {}

    def begin(kind, p, c):
        whole, masks = kinds[kind][2], kinds[kind][3]
        rounds[kind, p, c] = [
            (jnp.bitwise_xor(index, masks[p]), exchange(source, whole, index, c, masks[p], send_p.at[kind, c, (1 << p) - 2 + n], recv_p.at[kind, c, (1 << p) - 2 + n]))
            for n, (index, source) in enumerate(waiting[kind][c])
        ]

    def cross(kind, index, source, c, number):
        crossing.append(exchange(source, kinds[kind][2], index, c, 1, send_c.at[kind, c, number], recv_c.at[kind, c, number]))

    def begin_some(some):
        for c in some:
            for kind in range(2):
                if bits > 1:
                    begin(kind, 1, c)

    begin_some(range(EARLY))
    for c in range(nt):
        for kind in range(2):
            for n, (index, source) in enumerate(waiting[kind][c]):
                copy = pltpu.make_async_copy(source, kinds[kind][2].at[index, c], local.at[kind, c, n])
                copy.start()
                copies.append(copy)
                cross(kind, index, source, c, n)
    for i, item in enumerate(passes):
        for j in range(STATE_PARTS):
            item.arrive(j)
            helds[i][:, columns(j)] = join(sources[i][:, columns(j)], buffers[i][:, columns(j)])
        following = passes[i + 1 : i + 2] or ends
        for j in range(STATE_PARTS):
            for other in following:
                other.start(j)
    begin_some(range(EARLY, nt))
    for p in range(1, bits):
        for c in range(nt):
            for kind in range(2):
                for n, (index, copy) in enumerate(rounds[kind, p, c]):
                    copy.wait_recv()
                    source = kinds[kind][2].at[index, c]
                    waiting[kind][c].append((index, source))
                    cross(kind, index, source, c, (1 << p) + n)
                if p + 1 < bits:
                    begin(kind, p + 1, c)
    for j in range(STATE_PARTS):
        for item in ends:
            item.arrive(j)
        value = buffers[len(steps)][:, columns(j)]
        if far_step:
            value = join(value, buffers[len(steps) + 1][:, columns(j)])
        incoming[:, columns(j)] = value
    for copy in crossing:
        copy.wait_recv()
    for copy in copies:
        copy.wait()
    for item in passes + ends:
        item.finish()
    for copy in sent:
        copy.wait_send()


def spread(state, z_line, z_first, o_line, o_first, nw, span):
    nt, k, cols = z_line.shape
    nm = nw // 2
    steps, far_step = span_shifts(span)
    levels = len(steps) + 1 + (1 if far_step else 0)
    dma = pltpu.SemaphoreType.DMA
    vmem, anywhere = pl.BlockSpec(memory_space=pltpu.VMEM), pl.BlockSpec(memory_space=pl.ANY)
    return pl.pallas_call(
        functools.partial(spread_kernel, span=span),
        in_specs=[vmem] * 5,
        out_specs=[vmem, anywhere, anywhere],
        out_shape=[SDS(state.shape, BF), SDS((nw, nt, k, cols), BF), SDS((nw, nt, k, cols), BF)],
        scratch_shapes=[pltpu.VMEM(state.shape, BF)] * (levels + len(steps))
        + [dma((levels, STATE_PARTS))] * 2
        + [dma((2, nt, max(nm - 2, 1)))] * 2
        + [dma((2, nt, nm))] * 2
        + [dma((2, nt, 2))],
        compiler_params=params(48, collective_id=1, has_side_effects=True),
        cost_estimate=cost(60e9, 1e6),
        name="spread",
    )(state, z_line, z_first, o_line, o_first)


ROW_PARTS = 2
STEP_LAG = 4
SUM_GAP = 2


class Unit:
    def __init__(self, order, first, keep, kept, sends, recvs, send_sem, recv_sem, done):
        self.order, self.first, self.keep, self.kept, self.sends, self.recvs = order, first, keep, kept, sends, recvs
        self.send_sem, self.recv_sem, self.done = send_sem, recv_sem, done

    def copy(self, p):
        peer = {"wide": jnp.bitwise_xor(lax.axis_index("wide"), 2 << self.order[p])}
        return remote(self.sends[p], self.recvs[p], self.send_sem.at[p], self.recv_sem.at[p], peer)

    def merge(self, p):
        self.copy(p).wait_recv()
        keep = self.keep if p == self.first else self.kept
        count = self.recvs[p].shape[0]
        if p == len(self.order) - 1:
            self.done(keep[0].astype(F32) + self.recvs[p][0].astype(F32))
            return
        for i in range(count // 2):
            self.kept[i] = keep[i].astype(F32) + self.recvs[p][i].astype(F32)
        for i in range(count // 2, count):
            self.sends[p + 1][i - count // 2] = (keep[i].astype(F32) + self.recvs[p][i].astype(F32)).astype(BF)


def finish_kernel(
    dx, small, tail, tail_bc, rim, rim_bc, left, left_next, keep_a, send_a, keep_b, send_b, wx, so_far, tokens, cot, gain, conv_grad, gate_sums, bc_grad, head_grad,
    x_out, bc_out, dt_out, z_out, o_out, grad, sums_out, gain_out,
    dxs, dxn, smalls, smalln, rims, rims_bc, extra, weights,
    keep_x, send_x, recv_x, turn_x, own_x, got_x, kept_zo, send_zo, recv_zo, turn_zo, own_zo, got_zo, sums_to, sums_from, gain_to, gain_from,
    sem_flip, sem_rim, sem_local, sem_xs, sem_xr, sem_zs, sem_zr, sem_txs, sem_txr, sem_tzs, sem_tzr, sem_ss, sem_sr, sem_gs, sem_gr,
):
    nw, nt, k, cols = wx.shape
    rows, depth = tokens.shape
    block = INNER // nt
    nm = nw // 2
    bits = nm.bit_length() - 1
    per = nt // 2
    w, rank = lax.axis_index("wide"), lax.axis_index("tp")
    chip, core = w // 2, lax.rem(w, 2)
    count = nw * nt
    place = w * nt + rank
    before, behind = lax.rem(place + count - 1, count), lax.rem(place + 1, count)
    sibling = {"wide": jnp.bitwise_xor(w, 1)}
    tp_bits = nt.bit_length() - 1
    across = [{"tp": jnp.bitwise_xor(rank, 1 << b)} for b in range(tp_bits)]
    has_next = place < count - 1
    has_last = place > 0
    to_last = {"wide": before // nt, "tp": lax.rem(before, nt)}
    to_next = {"wide": behind // nt, "tp": lax.rem(behind, nt)}
    orders = (list(range(bits)), list(range(bits - 1, -1, -1)))

    @pl.when(jnp.logical_not(has_next))
    def _():
        rims[...] = jnp.zeros_like(rims)
        rims_bc[...] = jnp.zeros_like(rims_bc)

    greet([sibling, to_last, to_next] + across + [{"wide": jnp.bitwise_xor(w, 2 << b)} for b in range(bits)])
    rim_copies = [
        remote(rim, rims, sem_rim.at[0], sem_rim.at[1], to_last),
        remote(rim_bc, rims_bc, sem_rim.at[2], sem_rim.at[3], to_last),
    ]

    @pl.when(has_last)
    def _():
        for copy in rim_copies:
            copy.start()

    started = []

    def start(copy):
        copy.start()
        started.append(copy)

    body = pl.ds(0, rows - HALO)
    flips, locals_ = [], []
    order_of_turns = [turn for pair in zip(range(per - 1, -1, -1), range(nt - 1, per - 1, -1)) for turn in pair]
    small_copy = remote(small.at[body], smalln.at[body], sem_flip.at[0, 0], sem_flip.at[1, 0], sibling)
    start(small_copy)
    own_small = pltpu.make_async_copy(small, smalls, sem_local.at[nt])
    own_small.start()
    for n, turn in enumerate(order_of_turns):
        at = pl.ds(pl.multiple_of(jnp.bitwise_xor(rank, turn) * block, block), block)
        flips.append(remote(dx.at[body, at], dxn.at[body, at], sem_flip.at[0, 1 + n], sem_flip.at[1, 1 + n], sibling))
        start(flips[n])
        locals_.append(pltpu.make_async_copy(dx.at[:, at], dxs.at[:, at], sem_local.at[n]))
        locals_[n].start()
    initial = pltpu.make_async_copy(so_far, grad, sem_local.at[nt + 1])
    initial.start()

    def weight_copy(t):
        return pltpu.make_async_copy(wx.at[:, t], weights.at[t % 2], sem_local.at[nt + 2 + t % 2])

    weight_copy(0).start()

    def level(turn):
        return (turn & -turn).bit_length() - 1

    def finished(total, turn, own, leaving):
        if turn % 2:
            leaving[turn] = total.astype(BF)
        else:
            own[turn // 2] = total

    units_zo = []
    for q in range(2):
        for h, (keep, send) in enumerate(((keep_a, send_a), (keep_b, send_b))):
            def done(total, q=q, h=h):
                for i in range(per):
                    finished(total[:, i * block : (i + 1) * block], h * per + i, own_zo.at[q], turn_zo.at[q])

            number = 2 * q + h
            sends = {p: (send.at[q] if p == 1 else send_zo.at[number, pl.ds(0, nm >> (p + 1))]) for p in range(1, bits)}
            recvs = {p: recv_zo.at[number, pl.ds((nm >> 1) - (nm >> p), nm >> (p + 1))] for p in range(1, bits)}
            units_zo.append(
                Unit(orders[h], 1, keep.at[q], kept_zo.at[number], sends, recvs, sem_zs.at[number], sem_zr.at[number], done)
            )
    for unit in units_zo:
        start(unit.copy(1))

    part = k // ROW_PARTS
    units_x = []
    for s in range(ROW_PARTS):
        for turn in order_of_turns:
            number = len(units_x)

            def done(total, turn=turn, s=s):
                at = pl.ds(s * part, part)
                finished(total, turn, own_x.at[:, at], turn_x.at[:, at])

            sends = {p: send_x.at[number, pl.ds(nm - (nm >> p), nm >> (p + 1))] for p in range(bits)}
            recvs = {p: recv_x.at[number, pl.ds(nm - (nm >> p), nm >> (p + 1))] for p in range(bits)}
            unit = Unit(
                orders[0 if turn < per else 1], 0, keep_x.at[number], keep_x.at[number], sends, recvs, sem_xs.at[number], sem_xr.at[number], done
            )
            unit.turn, unit.s = turn, s
            units_x.append(unit)

    for copy in locals_:
        copy.wait()
    own_small.wait()

    @pl.when(has_next)
    def _():
        for copy in rim_copies:
            copy.wait_recv()

    last = slice(rows - HALO, rows)
    old = dxs[last].astype(F32)
    dxs[last] = jnp.concatenate([old[: HALO - 8], tail[...] + rims[...]], axis=0).astype(BF)
    old = smalls[last].astype(F32)
    fixed = jnp.concatenate([old[: HALO - 8, : 2 * STATE], tail_bc[...] + rims_bc[...]], axis=0)
    smalls[last] = jnp.concatenate([fixed, old[:, 2 * STATE :]], axis=1).astype(BF)

    end = pl.ds(rows - HALO, HALO)
    ends = [
        remote(smalls.at[end], smalln.at[end], sem_flip.at[0, nt + 1], sem_flip.at[1, nt + 1], sibling),
        remote(dxs.at[end], dxn.at[end], sem_flip.at[0, nt + 2], sem_flip.at[1, nt + 2], sibling),
    ]

    def members(order):
        found = []
        for index in range(nm // 2):
            r = 0
            for j, bit in enumerate(order[1:], 2):
                r |= ((index >> (len(order) - j)) & 1) << bit
            found.append(r)
        return found

    def compute(unit):
        order = unit.order
        kept = members(order)
        away = [r | (1 << order[0]) for r in kept]
        t = jnp.bitwise_xor(rank, unit.turn)
        at = pl.ds(pl.multiple_of(t * block, block), block)
        at_rows = pl.ds(unit.s * part, part)
        chips = [jnp.bitwise_xor(chip, r) for r in away + kept]
        places = [2 * m + core for m in chips]
        mine = jnp.concatenate([left[m, at_rows, :] for m in places], axis=0)
        theirs = jnp.concatenate([left_next[m, at_rows, :] for m in places], axis=0)
        result = mm(mine, dxs[:, at]) + mm(theirs, dxn[:, at])
        pick = select_columns(t, HEADS // nt, 2 * STATE // nt, cols - block, 2 * STATE + 128)
        picked = mm(jnp.concatenate([extra[m, at_rows, :] for m in chips], axis=0), pick, NT)
        value = jnp.concatenate([result, picked], axis=1)
        for i in range(nm // 2):
            unit.sends[0][i] = value[i * part : (i + 1) * part].astype(BF)
            unit.keep[i] = value[(nm // 2 + i) * part : (nm // 2 + i + 1) * part]

    def row_part(t):
        weight_copy(t).wait()
        if t + 1 < nt:
            weight_copy(t + 1).start()
        if t == 0:
            initial.wait()
        pick = select_columns(t, HEADS // nt, 2 * STATE // nt, cols - block, 2 * STATE + 128)
        extra_columns = mm(smalls[...], pick, NT).astype(BF)
        values = jnp.concatenate([dxs[:, t * block : (t + 1) * block], extra_columns], axis=1)
        grad[...] += mm(values, weights[t % 2].reshape(depth, cols), NT)

    def row_end():
        raw = tokens[...].astype(F32)
        inv = lax.rsqrt(jnp.mean(raw * raw, axis=-1, keepdims=True) + EPS)
        unit = raw * inv
        d_normed = grad[...]
        gain_grad = jnp.sum(d_normed * unit, axis=0, keepdims=True)
        gain_to[0] = gain_grad
        d_unit = d_normed * gain[...]
        grad[...] = cot[...].astype(F32) + inv * (d_unit - unit * jnp.mean(d_unit * unit, axis=-1, keepdims=True))

    partners = [{"wide": jnp.bitwise_xor(w, 1 << b)} for b in range(bits + 1)]
    partners += across

    def sum_start():
        sums_to[0, 0:5] = conv_grad[0:5]
        sums_to[0, 5:7] = gate_sums[0:2]
        for i in range(CONV + 1):
            sums_to[0, 7:8, i * 2 * STATE : (i + 1) * 2 * STATE] = bc_grad[i : i + 1]
        at = (CONV + 1) * 2 * STATE
        for i in range(2):
            sums_to[0, 7:8, at + i * 128 : at + (i + 1) * 128] = head_grad[i : i + 1]
        sums_to[0, 7:8, at + 256 :] = jnp.zeros((1, INNER - at - 256), F32)

    def butterfly(to, source, out, send, recv):
        def copy(i):
            return remote(to.at[i], source.at[i], send.at[i], recv.at[i], partners[i])

        def join(i):
            copy(i).wait_recv()
            total = to[i] + source[i]
            if i + 1 < len(partners):
                to[i + 1] = total
            else:
                out[...] = total

        return copy, join

    flies = [butterfly(sums_to, sums_from, sums_out, sem_ss, sem_sr), butterfly(gain_to, gain_from, gain_out, sem_gs, sem_gr)]

    def parcels(unit):
        if unit in units_zo:
            number = units_zo.index(unit)
            q, h = number // 2, number % 2
            for turn in range((h + 1) * per - 1, h * per - 1, -1):
                yield turn, own_zo.at[q], turn_zo.at[q], got_zo.at[q], sem_tzs.at[q], sem_tzr.at[q]
        else:
            at = pl.ds(unit.s * part, part)
            yield unit.turn, own_x.at[:, at], turn_x.at[:, at], got_x.at[:, :, at], sem_txs.at[unit.s], sem_txr.at[unit.s]

    def joined(turn, own, got, send, recv, upto):
        total = own[turn // 2]
        for b in range(upto):
            source = got.at[turn // 2, b]
            remote(source, source, send.at[turn], recv.at[turn // 2, b], across[b]).wait_recv()
            total = total + source[...].astype(F32)
        return total

    def pass_on(unit, odd):
        found = []
        for turn, own, leaving, got, send, recv in parcels(unit):
            if turn == 0 or bool(turn % 2) != odd:
                continue
            b = level(turn)
            if b:
                leaving[turn] = joined(turn, own, got, send, recv, b).astype(BF)
            target = turn ^ (1 << b)
            found.append(remote(leaving.at[turn], got.at[target // 2, b], send.at[turn], recv.at[target // 2, b], across[b]))
        return found

    side = [functools.partial(row_part, t) for t in range(nt)] + [row_end]
    total_x = len(units_x)
    steps = total_x + STEP_LAG * bits
    first_job = 1
    fly_steps = [
        [1 + SUM_GAP * i for i in range(len(partners) + 1)],
        [first_job + len(side) + i for i in range(len(partners) + 1)],
    ]
    steps = max(steps, fly_steps[0][-1], fly_steps[1][-1])
    later = {step: [] for step in range(steps + 2)}
    for step in range(steps + 1):
        ready = []
        leaving_now = [copy for unit in later[step] for copy in pass_on(unit, False)]
        if step < total_x:
            if step == 0:
                for copy in ends:
                    start(copy)
                small_copy.wait_recv()
                for copy in ends:
                    copy.wait_recv()
                small_all = [smalls[...], smalln[...]]
                for m in range(nm):
                    extra[m] = (mm(left[2 * m + core], small_all[0]) + mm(left_next[2 * m + core], small_all[1])).astype(BF)
            if step < len(flips):
                flips[step].wait_recv()
            compute(units_x[step])
        for p in range(bits - 1, -1, -1):
            u = step - STEP_LAG * (p + 1)
            if 0 <= u < total_x:
                units_x[u].merge(p)
                ready.append((units_x[u], p + 1))
        for p in range(bits - 1, 0, -1):
            u = step - 1 - STEP_LAG * (p - 1)
            if 0 <= u < len(units_zo):
                units_zo[u].merge(p)
                ready.append((units_zo[u], p + 1))
        if step == 0:
            sum_start()
        job = step - first_job
        if 0 <= job < len(side):
            side[job]()
        leaving_sums = []
        for (copy, join), when in zip(flies, fly_steps):
            if step in when:
                i = when.index(step)
                if i:
                    join(i - 1)
                if i < len(partners):
                    leaving_sums.append(copy(i))
        if step < total_x:
            start(units_x[step].copy(0))
        for unit, p in ready:
            if p < bits:
                start(unit.copy(p))
            else:
                for copy in pass_on(unit, True):
                    start(copy)
                later[step + 1].append(unit)
        for copy in leaving_now:
            start(copy)
        for copy in leaving_sums:
            start(copy)
    zo_total = []
    for q in range(2):
        unit = units_zo[2 * q]
        for turn, own, leaving, got, send, recv in parcels(unit):
            if turn == 0:
                zo_total.append(joined(0, own, got, send, recv, tp_bits))
    z_out[...] = zo_total[0]
    o_out[...] = zo_total[1].T
    for unit in units_x:
        for turn, own, leaving, got, send, recv in parcels(unit):
            if turn == 0:
                total = joined(0, own, got, send, recv, tp_bits)
                at = slice(unit.s * part, (unit.s + 1) * part)
                x_out[at] = total[:, :block]
                bc_out[at] = total[:, block : block + bc_out.shape[1]]
                dt_out[at] = total[:, block + bc_out.shape[1] : block + bc_out.shape[1] + dt_out.shape[1]]
    for copy in started:
        copy.wait_send()

    @pl.when(has_last)
    def _():
        for copy in rim_copies:
            copy.wait_send()


def finish(dx, small, tail, tail_bc, rim, rim_bc, left, left_next, keep_a, send_a, keep_b, send_b, wx, so_far, tokens, cot, gain, conv_grad, gate_sums, bc_grad, head_grad):
    nw, nt, k, cols = wx.shape
    rows, depth = tokens.shape
    nm = nw // 2
    bits = nm.bit_length() - 1
    block = INNER // nt
    half = nt // 2 * block
    part = k // ROW_PARTS
    units = ROW_PARTS * nt
    tp_bits = nt.bit_length() - 1
    partners = bits + 1 + tp_bits
    dma, vm = pltpu.SemaphoreType.DMA, pltpu.VMEM
    vmem, anywhere = pl.BlockSpec(memory_space=pltpu.VMEM), pl.BlockSpec(memory_space=pl.ANY)
    return pl.pallas_call(
        finish_kernel,
        in_specs=[anywhere, anywhere] + [vmem] * 6 + [vmem] * 4 + [anywhere, anywhere] + [vmem] * 7,
        out_specs=[vmem] * 8,
        out_shape=[
            SDS((k, block), F32), SDS((k, 2 * STATE // nt), F32), SDS((k, HEADS // nt), F32),
            SDS((k, block), F32), SDS((block, k), F32), SDS((rows, depth), F32), SDS((8, INNER), F32), SDS((1, depth), F32),
        ],
        scratch_shapes=[
            vm((rows, INNER), BF), vm((rows, INNER), BF), vm(small.shape, BF), vm(small.shape, BF),
            vm((8, INNER), F32), vm((8, 2 * STATE), F32), vm((nm, k, small.shape[1]), BF), vm((2, nw, k, cols), BF),
            vm((units, nm // 2, part, cols), F32), vm((units, nm - 1, part, cols), BF), vm((units, nm - 1, part, cols), BF),
            vm((nt, k, cols), BF), vm((nt // 2, k, cols), F32), vm((nt // 2, tp_bits, k, cols), BF),
            vm((4, nm // 4, k, half) if bits > 2 else (4, 1, 8, 128), F32),
            vm((4, nm // 8, k, half) if bits > 2 else (4, 1, 16, 128), BF),
            vm((4, max(nm // 2 - 1, 1), k, half), BF),
            vm((2, nt, k, block), BF), vm((2, nt // 2, k, block), F32), vm((2, nt // 2, tp_bits, k, block), BF),
            vm((partners, 8, INNER), F32), vm((partners, 8, INNER), F32), vm((partners, 1, depth), F32), vm((partners, 1, depth), F32),
            dma((2, nt + 3)), dma((4,)), dma((nt + 4,)),
            dma((units, bits)), dma((units, bits)), dma((4, bits)), dma((4, bits)),
            dma((ROW_PARTS, nt)), dma((ROW_PARTS, nt // 2, tp_bits)), dma((2, nt)), dma((2, nt // 2, tp_bits)),
            dma((partners,)), dma((partners,)), dma((partners,)), dma((partners,)),
        ],
        compiler_params=params(63, collective_id=2, has_side_effects=True),
        cost_estimate=cost(60e9, 1e6),
        name="finish",
    )(dx, small, tail, tail_bc, rim, rim_bc, left, left_next, keep_a, send_a, keep_b, send_b, wx, so_far, tokens, cot, gain, conv_grad, gate_sums, bc_grad, head_grad)


BOTH = ("wide", "tp")


def shift(value, steps):
    count = lax.axis_size("wide") * lax.axis_size("tp")
    first, last = max(0, -steps), min(count, count - steps)
    return lax.ppermute(value, BOTH, [(i, i + steps) for i in range(first, last)])


def carry_states(own, span, direction):
    reach = (DOC_MAX - 2) // span + 1
    held, size = own, 1
    while 2 * size < reach:
        other = shift(held, direction * size)
        held = combine(held, other)
        size *= 2
    near = shift(held, direction)
    if size >= reach:
        return near
    far = shift(held, direction * (1 + size))
    return combine(near, far)


def combine(near, far):
    decay = near[STATE : STATE + 1].astype(F32)
    state = near[:STATE].astype(F32) + decay * far[:STATE].astype(F32)
    whole = near[STATE:].astype(F32) * far[STATE:].astype(F32)
    return jnp.concatenate([state, whole], axis=0).astype(BF)


def flip(value, mask):
    return lax.ppermute(value, "wide", [(i, i ^ mask) for i in range(lax.axis_size("wide"))])


def add(a, b):
    return (a.astype(F32) + b.astype(F32)).astype(BF)


def first_exchange(keep_a, send_a, keep_b, send_b):
    top = keep_a.shape[1].bit_length() - 1
    size = keep_a.shape[1] // 2
    got_a, got_b = flip(send_a, 2), flip(send_b, 2 << top)
    result = []
    for keep, got in ((keep_a, got_a), (keep_b, got_b)):
        result += [add(keep[:, :size], got[:, :size]), add(keep[:, size:], got[:, size:])]
    return result


def per_device(
    tokens, segment_ids, out_cotangent, norm_gain, z_weight, x_weight, bc_weight, dt_weight, x_conv, x_bias,
    bc_conv, bc_bias, dt_bias, decay_log, skip_gain, gate_gain, out_weight,
):
    nw, nt = lax.axis_size("wide"), lax.axis_size("tp")
    rank = lax.axis_index("tp")
    rows, depth = tokens.shape
    k = depth // nw
    block = INNER // nt
    small = jnp.concatenate([bc_weight, dt_weight], axis=1)
    small = jnp.pad(small, ((0, 0), (0, 128 - small.shape[1])))
    own_x = jnp.concatenate([x_weight, small], axis=1)
    wx, z_line, o_line = gather(own_x, z_weight, out_weight.T, nw, nt)
    z_first, o_first = flip(z_line, 2), flip(o_line, nw // 2)

    own_ids = lax.dynamic_slice_in_dim(segment_ids, rank * rows, rows, 0)
    halo_rows = shift(tokens[rows - HALO :], 1)
    halo_ids = (shift(own_ids[rows - 128 :] + 1, 1) - 1).astype(F32)[None, :]
    row_ids = jnp.broadcast_to(own_ids.astype(F32)[None, :], (8, rows))

    def padded(v, width):
        v = v if v.ndim == 2 else v[None, :]
        return jnp.pad(v, ((0, 0), (0, width - v.shape[1])))

    wide_rows = jnp.concatenate(
        [x_conv, x_bias[None, :], jnp.repeat(skip_gain, HEAD_DIM)[None, :], gate_gain[None, :], x_bias[None, :]], axis=0
    ).astype(F32)
    small_rows = jnp.concatenate(
        [bc_conv, bc_bias[None, :], padded(dt_bias, 2 * STATE), padded(decay_log, 2 * STATE), bc_bias[None, :]], axis=0
    ).astype(F32)
    in_gain = norm_gain.astype(F32)[None, :]

    x_ext, misc, normed_ext, normed_t, info = project(tokens, halo_rows, in_gain, row_ids, halo_ids, wx)
    signal, y, own_state, ent, bc = ssd_forward(
        x_ext, misc, info, row_ids, wide_rows, small_rows
    )
    incoming, wz, wo = spread(own_state, z_line, z_first, o_line, o_first, nw, rows)
    core = lax.rem(lax.axis_index("wide"), 2)
    where = jnp.stack([lax.axis_index("wide") // 2, rank, core]).astype(jnp.int32)
    normed_next = flip(normed_t, 1).reshape(nw, k, rows)
    (gate,) = plain(normed_ext, wz, HALO, False)
    dno, cot_t = plain(out_cotangent, wo, 0, True)
    cot_next = flip(cot_t, 1).reshape(nw, k, rows)
    left = [normed_t.reshape(nw, k, rows), normed_next, cot_t.reshape(nw, k, rows), cot_next]
    pair, dy, adjoint, sums = gate_norm(y, signal, gate, dno, bc, ent, incoming, wide_rows)
    own_adjoint = jnp.concatenate([adjoint, own_state[STATE:]], axis=0)
    after = carry_states(own_adjoint, rows, -1)
    pair_next = flip(pair, 1)
    block_out = out_project(pair, wo, 0, tokens)
    so_far = gate_part(pair, wz, 0, depth)
    zo = weight_grad(where, left, pair, pair_next, nt, block)
    zo = first_exchange(*zo)
    dx, tail, rim, conv_grad, small_grad, tail_bc, rim_bc, bc_grad, head_grad = ssd_backward(
        x_ext, signal, dy, misc, info, row_ids, wide_rows, small_rows, incoming, after
    )
    x_weight_grad, bc_weight_grad, dt_weight_grad, z_weight_grad, out_weight_grad, grad_x, small_sums, gain_sum = finish(
        dx, small_grad, tail, tail_bc, rim, rim_bc, left[0], left[1], *zo, wx, so_far, tokens, out_cotangent, in_gain,
        conv_grad, sums, bc_grad, head_grad,
    )
    wide_bc = (CONV + 1) * 2 * STATE
    bc_all = small_sums[7, :wide_bc].reshape(CONV + 1, 2 * STATE)
    head_all = small_sums[7, wide_bc : wide_bc + 256]
    return (
        block_out,
        grad_x,
        gain_sum[0],
        z_weight_grad,
        x_weight_grad,
        bc_weight_grad,
        dt_weight_grad,
        small_sums[:CONV],
        small_sums[CONV],
        bc_all[:CONV],
        bc_all[CONV],
        head_all[:HEADS],
        head_all[128 : 128 + HEADS],
        small_sums[6].reshape(HEADS, HEAD_DIM).sum(axis=1),
        small_sums[5],
        out_weight_grad,
    )


def solution(mesh):
    rows, shard, out_shard = P(("wide", "tp"), None), P("wide", "tp"), P("tp", "wide")
    return jax.shard_map(
        per_device,
        mesh=mesh,
        in_specs=(rows, P("wide"), rows, P(), shard, shard, shard, shard) + (P(),) * 8 + (out_shard,),
        out_specs=(rows, rows, P(), shard, shard, shard, shard) + (P(),) * 8 + (out_shard,),
        check_vma=False,
    )
```

profile of v0, /device:TPU:4, one launch (start us, length us, event | category | flops | bytes accessed | tf_op | source)
XLA Modules:
  0.0 561.8 jit_solution(3558239250651280708)
XLA Ops:
  2.1 3.5 collective-permute-start
  6.8 3.5 collective-permute-start.1
  15.0 69.3 %gather.1 = (bf16[8,4,192,896]{3,2,1,0:T(8,128)(2,1)S(1)}, bf16[4,192,768]{2,1,0:T(8,128)(2,1)S(1)}, bf16[4,192,768]{2,1,0:T(8,128)(2,1)S(1)}) custom-call(bf16[192,896]{1,0:T(8,128)(2,1)S(1)} %pad_maximum_fusion.3.own, bf16[192,768]{1,0:T(8,128)(2,1)S(1)} %copy-done.1, bf16[192,768]{1,0:T(8,128)(2,1)S(1)} %bitcast.21), custom_call_target="tpu_custom_call" | custom-call | flops 60000002048 | bytes 1000000 | tf_op jit(solution)/shard_map/gather/pallas_call | solution.py:941
  84.3 4.2 copy-done.3
  94.5 1.5 concatenate.25
  96.0 1.4 convert_element_type.84.wide_rows
  103.1 12.4 %project.1 = (bf16[528,3072]{1,0:T(8,128)(2,1)}, bf16[4,528,128]{2,1,0:T(8,128)(2,1)}, bf16[528,1536]{1,0:T(8,128)(2,1)}, bf16[1536,512]{1,0:T(8,128)(2,1)}, f32[512,8]{1,0:T(8,128)}) custom-call(bf16[512,1536]{1,0:T(8,128)(2,1)} %tokens.3, bf16[16,1536]{1,0:T(8,128)(2,1)} %collective-permute-done.halo, f32[1,1536]{1,0:T(1,128)} %reshape.54.gain, ...), custom_call_target="tpu_custom_call" | custom-call | flops 5813305344 | bytes 11010048 | tf_op jit(solution)/shard_map/project/pallas_call | solution.py:100
  115.5 19.6 %ssd_forward.1 = (bf16[512,3072]{1,0:T(8,128)(2,1)}, bf16[512,3072]{1,0:T(8,128)(2,1)}, bf16[144,3072]{1,0:T(8,128)(2,1)}, f32[512,128]{1,0:T(8,128)}, bf16[512,256]{1,0:T(8,128)(2,1)}) custom-call(bf16[528,3072]{1,0:T(8,128)(2,1)} %get-tuple-element.60.x, bf16[4,528,128]{2,1,0:T(8,128)(2,1)} %get-tuple-element.61.misc, f32[512,8]{1,0:T(8,128)} %get-tuple-element.62.info, ...), custom_call_target="tpu_custom_call" | custom-call | flops 20000000000 | bytes 12000000 | tf_op jit(solution)/shard_map/ssd_forward/pallas_call | solution.py:308
  137.2 88.6 %spread.1 = (bf16[144,3072]{1,0:T(8,128)(2,1)S(1)}, bf16[8,4,192,768]{3,2,1,0:T(8,128)(2,1)}, bf16[8,4,192,768]{3,2,1,0:T(8,128)(2,1)}) custom-call(bf16[144,3072]{1,0:T(8,128)(2,1)S(1)} %copy-done, bf16[4,192,768]{2,1,0:T(8,128)(2,1)S(1)} %get-tuple-element.67.z_line, bf16[4,192,768]{2,1,0:T(8,128)(2,1)S(1)} %collective-permute-done.2.z_first, ...), custom_call_target="tpu_custom_call" | custom-call | flops 60000002048 | bytes 1000000 | tf_op jit(solution)/shard_map/spread/pallas_call | solution.py:1139
  226.8 9.4 %shard_map.288.gate = bf16[512,3072]{1,0:T(8,128)(2,1)} custom-call(bf16[528,1536]{1,0:T(8,128)(2,1)} %get-tuple-element.65.left, bf16[8,4,192,768]{3,2,1,0:T(8,128)(2,1)} %get-tuple-element.69.weight), custom_call_target="tpu_custom_call" | custom-call | flops 4831838208 | bytes 9437184 | tf_op jit(solution)/shard_map/pallas_call | solution.py:151
  236.2 9.8 %shard_map.289 = (bf16[512,3072]{1,0:T(8,128)(2,1)}, bf16[1536,512]{1,0:T(8,128)(2,1)}) custom-call(bf16[512,1536]{1,0:T(8,128)(2,1)} %cot.1, bf16[8,4,192,768]{3,2,1,0:T(8,128)(2,1)} %get-tuple-element.70.weight), custom_call_target="tpu_custom_call" | custom-call | flops 4831838208 | bytes 9437184 | tf_op jit(solution)/shard_map/pallas_call | solution.py:151
  246.0 22.4 %gate_norm.1 = (bf16[2,512,3072]{2,1,0:T(8,128)(2,1)}, bf16[512,3072]{1,0:T(8,128)(2,1)}, bf16[128,3072]{1,0:T(8,128)(2,1)}, f32[8,3072]{1,0:T(8,128)}) custom-call(bf16[512,3072]{1,0:T(8,128)(2,1)} %get-tuple-element.63.y, bf16[512,3072]{1,0:T(8,128)(2,1)} %get-tuple-element.64.signal, bf16[512,3072]{1,0:T(8,128)(2,1)} %shard_map.288.gate, ...), custom_call_target="tpu_custom_call" | custom-call | flops 10000000000 | bytes 25000000 | tf_op jit(solution)/shard_map/gate_norm/pallas_call | solution.py:420
  270.2 1.9 collective-permute-start.4
  274.0 19.7 %collective-permute-done.4 = bf16[144,3072]{1,0:T(8,128)(2,1)S(1)} collective-permute-done((bf16[144,3072]{1,0:T(8,128)(2,1)S(1)}, bf16[144,3072]{1,0:T(8,128)(2,1)S(1)}, u32[]{:S(2)}, u32[]{:S(2)}) %collective-permute-start.4) | collective-permute-done | bytes 884768 | tf_op jit(solution)/shard_map/ppermute | solution.py:1560
  294.9 1.9 collective-permute-start.6
  296.9 5.4 collective-permute-start.5
  302.3 10.8 %out_project.1 = bf16[512,1536]{1,0:T(8,128)(2,1)} custom-call(bf16[2,512,3072]{2,1,0:T(8,128)(2,1)} %get-tuple-element.75.left.own, bf16[8,4,192,768]{3,2,1,0:T(8,128)(2,1)} %get-tuple-element.70.weight, bf16[512,1536]{1,0:T(8,128)(2,1)} %tokens.3), custom_call_target="tpu_custom_call" | custom-call | flops 4831838208 | bytes 9437184 | tf_op jit(solution)/shard_map/out_project/pallas_call | solution.py:741
  313.1 10.6 %gate_part.1.so_far = f32[512,1536]{1,0:T(8,128)} custom-call(bf16[2,512,3072]{2,1,0:T(8,128)(2,1)} %get-tuple-element.75.left.own, bf16[8,4,192,768]{3,2,1,0:T(8,128)(2,1)} %get-tuple-element.69.weight), custom_call_target="tpu_custom_call" | custom-call | flops 4831838208 | bytes 9437184 | tf_op jit(solution)/shard_map/gate_part/pallas_call | solution.py:776
  323.6 14.7 %collective-permute-done.5 = bf16[144,3072]{1,0:T(8,128)(2,1)S(1)} collective-permute-done((bf16[144,3072]{1,0:T(8,128)(2,1)S(1)}, bf16[144,3072]{1,0:T(8,128)(2,1)S(1)}, u32[]{:S(2)}, u32[]{:S(2)}) %collective-permute-start.5) | collective-permute-done | bytes 884768 | tf_op jit(solution)/shard_map/ppermute | solution.py:1560
  339.6 22.1 %shard_map.290 = (bf16[2,2,192,1536]{3,2,1,0:T(8,128)(2,1)}, bf16[2,2,192,1536]{3,2,1,0:T(8,128)(2,1)}, bf16[2,2,192,1536]{3,2,1,0:T(8,128)(2,1)}, bf16[2,2,192,1536]{3,2,1,0:T(8,128)(2,1)}) custom-call(s32[3]{0:T(128)} %pad_add_fusion.where, bf16[8,192,512]{2,1,0:T(8,128)(2,1)} %bitcast.29, bf16[8,192,512]{2,1,0:T(8,128)(2,1)} %bitcast.7.next_z.left_next, ...), custom_call_target="tpu_custom_call" | custom-call | flops 9663676416 | bytes 28311552 | tf_op jit(solution)/shard_map/pallas_call | solution.py:705
  361.8 1.7 collective-permute-start.11
  363.5 42.5 %ssd_backward.1 = (bf16[512,3072]{1,0:T(8,128)(2,1)}, f32[8,3072]{1,0:T(8,128)}, f32[8,3072]{1,0:T(8,128)}, f32[8,3072]{1,0:T(8,128)}, bf16[512,384]{1,0:T(8,128...) custom-call(bf16[528,3072]{1,0:T(8,128)(2,1)} %get-tuple-element.60.x, ...), custom_call_target="tpu_custom_call" | custom-call | flops 40000000000 | bytes 15000000 | tf_op jit(solution)/shard_map/ssd_backward/pallas_call | solution.py:592
  406.0 9.3 %collective-permute-done.10 = bf16[2,2,192,1536]{3,2,1,0:T(8,128)(2,1)} collective-permute-done((bf16[2,2,192,1536]{3,2,1,0:T(8,128)(2,1)}, bf16[2,2,192,1536]{3,2,1,0:T(8,128)(2,1)}, u32[]{:S(2)}, u32[]{:S(2)}) %collective-permute-start.10) | collective-permute-done | bytes 2359328 | tf_op jit(solution)/shard_map/ppermute | solution.py:1585
  415.3 3.8 add_convert_fusion.2
  419.1 3.7 add_convert_fusion
  422.7 119.3 %finish.1 = (f32[192,768]{1,0:T(8,128)}, f32[192,64]{1,0:T(8,128)}, f32[192,12]{1,0:T(8,128)}, f32[192,768]{1,0:T(8,128)}, f32[768,192]{1,0:T(8,128)}, /*index=5...) custom-call(bf16[512,3072]{1,0:T(8,128)(2,1)} %get-tuple-element.78.dx, ...), custom_call_target="tpu_custom_call" | custom-call | flops 60000002048 | bytes 1000000 | tf_op jit(solution)/shard_map/finish/pallas_call | solution.py:1525
  542.1 1.5 slice.117
  543.6 1.7 fusion.4
  548.5 1.6 copy.35
  550.1 1.6 copy.36
  552.4 2.2 copy.37
  555.8 3.9 copy.41
  (81 shorter events, 35.0 us)
Async XLA Ops:
  2.1 100.4 %collective-permute-start = (bf16[16,1536]{1,0:T(8,128)(2,1)}, bf16[16,1536]{1,0:T(8,128)(2,1)}, u32[]{:S(2)}, u32[]{:S(2)}) collective-permute-start(bf16[16,1536]{1,0:T(8,128)(2,1)} %slice.98), channel_id=1, source_target_pairs={{0,1},{1,2},{2,3},{3,4},{4,5},{5,6},{6,7},{7,8},{8,9},{9,10},{10,1... | collective-permute-start | bytes 147464 | tf_op jit(solution)/shard_map/ppermute | solution.py:1560
  6.8 94.5 %collective-permute-start.1 = (s32[128]{0:T(128)}, s32[128]{0:T(128)}, u32[]{:S(2)}, u32[]{:S(2)}) collective-permute-start(s32[128]{0:T(128)} %slice_add_fusion), channel_id=1, source_target_pairs={{0,1},{1,2},{2,3},{3,4},{4,5},{5,6},{6,7},{7,8},{8,9},{9,10},{10,1... | collective-permute-start | bytes 1544 | tf_op jit(solution)/shard_map/ppermute | solution.py:1560
  13.1 1.0 copy-start.1
  14.1 1.0 copy-start.2
  15.0 75.5 %copy-start.12 = (bf16[1536]{0:T(1024)(128)(2,1)S(1)}, bf16[1536]{0:T(1024)(128)(2,1)}, u32[]{:S(2)}) copy-start(bf16[1536]{0:T(1024)(128)(2,1)} %param.20) | copy-start | bytes 9220
  15.0 76.1 %copy-start.10 = (bf16[3072]{0:T(1024)(128)(2,1)S(1)}, bf16[3072]{0:T(1024)(128)(2,1)}, u32[]{:S(2)}) copy-start(bf16[3072]{0:T(1024)(128)(2,1)} %param.26) | copy-start | bytes 18436
  15.0 76.1 %copy-start.13 = (bf16[48]{0:T(256)(128)(2,1)S(1)}, bf16[48]{0:T(256)(128)(2,1)}, u32[]{:S(2)}) copy-start(bf16[48]{0:T(256)(128)(2,1)} %param.31) | copy-start | bytes 292
  84.3 4.2 copy-start.3
  88.5 47.5 %collective-permute-start.2 = (bf16[4,192,768]{2,1,0:T(8,128)(2,1)S(1)}, bf16[4,192,768]{2,1,0:T(8,128)(2,1)S(1)}, u32[]{:S(2)}, u32[]{:S(2)}) collective-permute-start(bf16[4,192,768]{2,1,0:T(8,128)(2,1)S(1)} %get-tuple-element.67.z_line), channel_id=1, source_target_pairs={{0,8},{4,12},{8,0},{12,4},{16,24},{20,28},{24,16},{28,20},{1,9},{5... | collective-permute-start | bytes 3538952 | tf_op jit(solution)/shard_map/ppermute | solution.py:1585
  89.5 46.5 %collective-permute-start.3 = (bf16[4,192,768]{2,1,0:T(8,128)(2,1)S(1)}, bf16[4,192,768]{2,1,0:T(8,128)(2,1)}, u32[]{:S(2)}, u32[]{:S(2)}) collective-permute-start(bf16[4,192,768]{2,1,0:T(8,128)(2,1)S(1)} %get-tuple-element.68.o_line), channel_id=1, source_target_pairs={{0,16},{4,20},{8,24},{12,28},{16,0},{20,4},{24,8},{28,12},{1,17},{... | collective-permute-start | bytes 3538952 | tf_op jit(solution)/shard_map/ppermute | solution.py:1585
  136.0 1.2 copy-start
  225.8 0.9 copy-start.4
  268.4 26.2 %copy-start.5 = (bf16[128,3072]{1,0:T(8,128)(2,1)S(1)}, bf16[128,3072]{1,0:T(8,128)(2,1)}, u32[]{:S(2)}) copy-start(bf16[128,3072]{1,0:T(8,128)(2,1)} %get-tuple-element.77) | copy-start | bytes 2359300
  268.4 71.2 %collective-permute-start.9 = (bf16[2,512,3072]{2,1,0:T(8,128)(2,1)}, bf16[2,512,3072]{2,1,0:T(8,128)(2,1)}, u32[]{:S(2)}, u32[]{:S(2)}) collective-permute-start(bf16[2,512,3072]{2,1,0:T(8,128)(2,1)} %get-tuple-element.75.left.own), channel_id=1, source_target_pairs={{0,4},{4,0},{8,12},{12,8},{16,20},{20,16},{24,28},{28,24},{1,5},{5... | collective-permute-start | bytes 18874376 | tf_op jit(solution)/shard_map/ppermute | solution.py:1585
  270.2 23.5 %collective-permute-start.4 = (bf16[144,3072]{1,0:T(8,128)(2,1)S(1)}, bf16[144,3072]{1,0:T(8,128)(2,1)S(1)}, u32[]{:S(2)}, u32[]{:S(2)}) collective-permute-start(bf16[144,3072]{1,0:T(8,128)(2,1)S(1)} %pad_maximum_fusion), channel_id=1, source_target_pairs={{1,0},{2,1},{3,2},{4,3},{5,4},{6,5},{7,6},{8,7},{9,8},{10,9},{11,1... | collective-permute-start | bytes 2654216 | tf_op jit(solution)/shard_map/ppermute | solution.py:1560
  272.7 67.0 %collective-permute-start.7 = (bf16[1536,512]{1,0:T(8,128)(2,1)}, bf16[1536,512]{1,0:T(8,128)(2,1)}, u32[]{:S(2)}, u32[]{:S(2)}) collective-permute-start(bf16[1536,512]{1,0:T(8,128)(2,1)} %get-tuple-element.84), channel_id=1, source_target_pairs={{0,4},{4,0},{8,12},{12,8},{16,20},{20,16},{24,28},{28,24},{1,5},{5... | collective-permute-start | bytes 4718600 | tf_op jit(solution)/shard_map/ppermute | solution.py:1585
  273.6 66.1 %collective-permute-start.8 = (bf16[1536,512]{1,0:T(8,128)(2,1)}, bf16[1536,512]{1,0:T(8,128)(2,1)}, u32[]{:S(2)}, u32[]{:S(2)}) collective-permute-start(bf16[1536,512]{1,0:T(8,128)(2,1)} %get-tuple-element.85), channel_id=1, source_target_pairs={{0,4},{4,0},{8,12},{12,8},{16,20},{20,16},{24,28},{28,24},{1,5},{5... | collective-permute-start | bytes 4718600 | tf_op jit(solution)/shard_map/ppermute | solution.py:1585
  294.9 28.7 %collective-permute-start.6 = (bf16[144,3072]{1,0:T(8,128)(2,1)S(1)}, bf16[144,3072]{1,0:T(8,128)(2,1)S(1)}, u32[]{:S(2)}, u32[]{:S(2)}) collective-permute-start(bf16[144,3072]{1,0:T(8,128)(2,1)S(1)} %pad_maximum_fusion.1), channel_id=1, source_target_pairs={{3,0},{4,1},{5,2},{6,3},{7,4},{8,5},{9,6},{10,7},{11,8},{12,9},{13... | collective-permute-start | bytes 2654216 | tf_op jit(solution)/shard_map/ppermute | solution.py:1560
  296.9 41.5 %collective-permute-start.5 = (bf16[144,3072]{1,0:T(8,128)(2,1)S(1)}, bf16[144,3072]{1,0:T(8,128)(2,1)S(1)}, u32[]{:S(2)}, u32[]{:S(2)}) collective-permute-start(bf16[144,3072]{1,0:T(8,128)(2,1)S(1)} %pad_maximum_fusion.1), channel_id=1, source_target_pairs={{1,0},{2,1},{3,2},{4,3},{5,4},{6,5},{7,6},{8,7},{9,8},{10,9},{11,1... | collective-permute-start | bytes 2654216 | tf_op jit(solution)/shard_map/ppermute | solution.py:1560
  361.8 53.5 %collective-permute-start.10 = (bf16[2,2,192,1536]{3,2,1,0:T(8,128)(2,1)}, bf16[2,2,192,1536]{3,2,1,0:T(8,128)(2,1)}, u32[]{:S(2)}, u32[]{:S(2)}) collective-permute-start(bf16[2,2,192,1536]{3,2,1,0:T(8,128)(2,1)} %get-tuple-element.87), channel_id=1, source_target_pairs={{0,8},{4,12},{8,0},{12,4},{16,24},{20,28},{24,16},{28,20},{1,9},{5... | collective-permute-start | bytes 7077896 | tf_op jit(solution)/shard_map/ppermute | solution.py:1585
  361.8 57.3 %collective-permute-start.11 = (bf16[2,2,192,1536]{3,2,1,0:T(8,128)(2,1)}, bf16[2,2,192,1536]{3,2,1,0:T(8,128)(2,1)}, u32[]{:S(2)}, u32[]{:S(2)}) collective-permute-start(bf16[2,2,192,1536]{3,2,1,0:T(8,128)(2,1)} %get-tuple-element.89), channel_id=1, source_target_pairs={{0,16},{4,20},{8,24},{12,28},{16,0},{20,4},{24,8},{28,12},{1,17},{... | collective-permute-start | bytes 7077896 | tf_op jit(solution)/shard_map/ppermute | solution.py:1585
  363.5 51.7 %copy-start.7 = (bf16[2,2,192,1536]{3,2,1,0:T(8,128)(2,1)S(1)}, bf16[2,2,192,1536]{3,2,1,0:T(8,128)(2,1)}, u32[]{:S(2)}) copy-start(bf16[2,2,192,1536]{3,2,1,0:T(8,128)(2,1)} %get-tuple-element.86) | copy-start | bytes 7077892
  415.3 3.8 copy-start.6
  542.1 12.5 %copy-start.11 = (f32[1,1536]{1,0:T(1,128)S(1)}, f32[1,1536]{1,0:T(1,128)}, u32[]{:S(2)}) copy-start(f32[1,1536]{1,0:T(1,128)} %get-tuple-element.95) | copy-start | bytes 18436
  555.8 3.9 copy-start.9
  555.8 4.7 copy-start.8
where the time goes:
time: 569 us; the launch traced here: 562 us
  Pallas kernels  437 us (77%)
  waiting for transfers between devices  43.7 us (8%)
  local copies, waits for them, and re-layouts  39.5 us (7%)
  starting transfers between devices  21 us (4%)
  other arithmetic  19.4 us (3%)
    pallas_call x1, Pallas kernels, finish(): pl.pallas_call(finish_kernel, in_specs=[anywhere, anywhere] + [vmem] * 6...  119 us
    pallas_call x1, Pallas kernels, spread(): pl.pallas_call(functools.partial(spread_kernel, span=span), in_specs=[vme...  88.6 us
    pallas_call x1, Pallas kernels, gather(): pl.pallas_call(gather_kernel, in_specs=[pl.BlockSpec(memory_space=pltpu.V...  69.3 us
    pallas_call x1, Pallas kernels, ssd_backward(): pl.pallas_call(ssd_back_kernel, grid=(INNER // LANES,), in_specs=[column_...  42.5 us
    ppermute x5, waiting for transfers between devices, shift(): lax.ppermute(value, BOTH, [(i, i + steps) for i in range(first, last)])  34.4 us
    pallas_call x1, Pallas kernels, gate_norm(): pl.pallas_call(gate_kernel, grid=(rows // size,), in_specs=[row(INNER), r...  22.4 us
    pallas_call x1, Pallas kernels, weight_grad(): pl.pallas_call(functools.partial(weight_grad_body, cols=cols, top=nm.bit_...  22.1 us
    unnamed x36, local copies, waits for them, and re-layouts  20.8 us
  transfers between devices with their start and end apart: 12, of which 3 were waited for; matrix products, arithmetic and copies ran while one was open for 5% of the time, Pallas kernels for 29%

commit v1 on v0

--- a/solution.py
+++ b/solution.py
@@ -74,15 +74,15 @@
     return result
 
 
-def proj_kernel(tok, halo, gain, ids, halo_ids, weight, x_out, misc_out, normed, turned, info):
+def proj_kernel(tok, halo, gain, ids, weight, x_out, misc_out, normed, turned, info):
     @pl.when(pl.program_id(0) == 0)
     def _():
         for rows, at in ((halo, slice(0, HALO)), (tok, slice(HALO, None))):
-            raw = rows[...].astype(F32)
+            raw = rows[...].astype(F32)[: rows.shape[0] if rows is tok else HALO]
             inv = lax.rsqrt(jnp.mean(raw * raw, axis=-1, keepdims=True) + EPS)
             normed[at] = (raw * inv * gain[...]).astype(BF)
         turned[...] = normed[HALO:].T
-        info[...] = marks_of(ids[...], halo_ids[...])
+        info[...] = marks_of(ids[...], halo[HALO:, 0:128].astype(F32)[0:1] - 1.0)
 
     depth, cols = tok.shape[1], weight.shape[3]
     result = mm(normed[...], weight[...].reshape(depth, cols))
@@ -91,7 +91,7 @@
     misc_out[0] = result[:, block:].astype(BF)
 
 
-def project(tokens, halo_rows, gain, ids, halo_ids, weights):
+def project(tokens, halo_rows, gain, ids, weights):
     rows, depth = tokens.shape
     rows = rows + HALO
     nw, nt, k, cols = weights.shape
@@ -105,7 +105,6 @@
             whole_spec(halo_rows.shape),
             whole_spec((1, depth)),
             whole_spec(ids.shape),
-            whole_spec(halo_ids.shape),
             pl.BlockSpec((nw, 1, k, cols), lambda t: (0, t, 0, 0)),
         ],
         out_specs=[
@@ -125,7 +124,7 @@
         compiler_params=params(),
         cost_estimate=cost(2 * rows * depth * nt * cols, 2 * depth * nt * cols),
         name="project",
-    )(tokens, halo_rows, gain, ids, halo_ids, weights)
+    )(tokens, halo_rows, gain, ids, weights)
 
 
 def plain_kernel(left, weight, out, *turned, first):
@@ -1615,8 +1614,8 @@
     z_first, o_first = flip(z_line, 2), flip(o_line, nw // 2)
 
     own_ids = lax.dynamic_slice_in_dim(segment_ids, rank * rows, rows, 0)
-    halo_rows = shift(tokens[rows - HALO :], 1)
-    halo_ids = (shift(own_ids[rows - 128 :] + 1, 1) - 1).astype(F32)[None, :]
+    last_ids = jnp.pad((own_ids[rows - 128 :] + 1).astype(BF)[None, :], ((0, HALO - 1), (0, depth - 128)))
+    halo_rows = shift(jnp.concatenate([tokens[rows - HALO :], last_ids], axis=0), 1)
     row_ids = jnp.broadcast_to(own_ids.astype(F32)[None, :], (8, rows))
 
     def padded(v, width):
@@ -1631,7 +1630,7 @@
     ).astype(F32)
     in_gain = norm_gain.astype(F32)[None, :]
 
-    x_ext, misc, normed_ext, normed_t, info = project(tokens, halo_rows, in_gain, row_ids, halo_ids, wx)
+    x_ext, misc, normed_ext, normed_t, info = project(tokens, halo_rows, in_gain, row_ids, wx)
     signal, y, own_state, ent, bc = ssd_forward(
         x_ext, misc, info, row_ids, wide_rows, small_rows
     )

time: 569 us -> 564 us (level)
  the two profiles are of different devices: /device:TPU:4 before, /device:TPU:8 now
where the time goes in v1:
time: 564 us; the launch traced here: 553 us
  Pallas kernels  422 us (75%)
  waiting for transfers between devices  42.7 us (8%)
  local copies, waits for them, and re-layouts  38.9 us (7%)
  starting transfers between devices  29.6 us (5%)
  other arithmetic  18.3 us (3%)
    pallas_call x1, Pallas kernels, finish(): pl.pallas_call(finish_kernel, in_specs=[anywhere, anywhere] + [vmem] * 6...  117 us
    pallas_call x1, Pallas kernels, spread(): pl.pallas_call(functools.partial(spread_kernel, span=span), in_specs=[vme...  78.6 us
    pallas_call x1, Pallas kernels, gather(): pl.pallas_call(gather_kernel, in_specs=[pl.BlockSpec(memory_space=pltpu.V...  66.7 us
    pallas_call x1, Pallas kernels, ssd_backward(): pl.pallas_call(ssd_back_kernel, grid=(INNER // LANES,), in_specs=[column_...  42.5 us
    ppermute x4, waiting for transfers between devices, shift(): lax.ppermute(value, BOTH, [(i, i + steps) for i in range(first, last)])  33.5 us
    ppermute x4, starting transfers between devices, shift(): lax.ppermute(value, BOTH, [(i, i + steps) for i in range(first, last)])  23.4 us
    pallas_call x1, Pallas kernels, gate_norm(): pl.pallas_call(gate_kernel, grid=(rows // size,), in_specs=[row(INNER), r...  22.4 us
    pallas_call x1, Pallas kernels, weight_grad(): pl.pallas_call(functools.partial(weight_grad_body, cols=cols, top=nm.bit_...  22.3 us
  transfers between devices with their start and end apart: 11, of which 3 were waited for; matrix products, arithmetic and copies ran while one was open for 4% of the time, Pallas kernels for 29%

profile of v1, /device:TPU:8, one launch (start us, length us, event | category | flops | bytes accessed | tf_op | source)
XLA Modules:
  0.0 552.8 jit_solution(18105088394622736715)
XLA Ops:
  2.9 3.5 collective-permute-start
  11.1 66.7 %gather.1 = (bf16[8,4,192,896]{3,2,1,0:T(8,128)(2,1)S(1)}, bf16[4,192,768]{2,1,0:T(8,128)(2,1)S(1)}, bf16[4,192,768]{2,1,0:T(8,128)(2,1)S(1)}) custom-call(bf16[192,896]{1,0:T(8,128)(2,1)S(1)} %pad_maximum_fusion.3.own, bf16[192,768]{1,0:T(8,128)(2,1)S(1)} %copy-done.1, bf16[192,768]{1,0:T(8,128)(2,1)S(1)} %bitcast.21), custom_call_target="tpu_custom_call" | custom-call | flops 60000002048 | bytes 1000000 | tf_op jit(solution)/shard_map/gather/pallas_call | solution.py:940
  77.8 4.2 copy-done.3
  82.0 2.0 collective-permute-start.1
  85.4 1.4 broadcast_in_dim_reshape.3
  88.1 1.5 concatenate.29
  89.6 1.4 convert_element_type.86.wide_rows
  95.5 12.4 %project.1 = (bf16[528,3072]{1,0:T(8,128)(2,1)}, bf16[4,528,128]{2,1,0:T(8,128)(2,1)}, bf16[528,1536]{1,0:T(8,128)(2,1)}, bf16[1536,512]{1,0:T(8,128)(2,1)}, f32[512,8]{1,0:T(8,128)}) custom-call(bf16[512,1536]{1,0:T(8,128)(2,1)} %tokens.3, bf16[32,1536]{1,0:T(8,128)(2,1)} %collective-permute-done.halo, f32[1,1536]{1,0:T(1,128)} %reshape.54.gain, ...), custom_call_target="tpu_custom_call" | custom-call | flops 5813305344 | bytes 11010048 | tf_op jit(solution)/shard_map/project/pallas_call | solution.py:100
  107.9 19.6 %ssd_forward.1 = (bf16[512,3072]{1,0:T(8,128)(2,1)}, bf16[512,3072]{1,0:T(8,128)(2,1)}, bf16[144,3072]{1,0:T(8,128)(2,1)}, f32[512,128]{1,0:T(8,128)}, bf16[512,256]{1,0:T(8,128)(2,1)}) custom-call(bf16[528,3072]{1,0:T(8,128)(2,1)} %get-tuple-element.60.x, bf16[4,528,128]{2,1,0:T(8,128)(2,1)} %get-tuple-element.61.misc, f32[512,8]{1,0:T(8,128)} %get-tuple-element.62.info, ...), custom_call_target="tpu_custom_call" | custom-call | flops 20000000000 | bytes 12000000 | tf_op jit(solution)/shard_map/ssd_forward/pallas_call | solution.py:307
  129.6 78.6 %spread.1 = (bf16[144,3072]{1,0:T(8,128)(2,1)S(1)}, bf16[8,4,192,768]{3,2,1,0:T(8,128)(2,1)}, bf16[8,4,192,768]{3,2,1,0:T(8,128)(2,1)}) custom-call(bf16[144,3072]{1,0:T(8,128)(2,1)S(1)} %copy-done, bf16[4,192,768]{2,1,0:T(8,128)(2,1)S(1)} %get-tuple-element.67.z_line, bf16[4,192,768]{2,1,0:T(8,128)(2,1)S(1)} %collective-permute-done.1.z_first, ...), custom_call_target="tpu_custom_call" | custom-call | flops 60000002048 | bytes 1000000 | tf_op jit(solution)/shard_map/spread/pallas_call | solution.py:1138
  209.1 9.3 %shard_map.288.gate = bf16[512,3072]{1,0:T(8,128)(2,1)} custom-call(bf16[528,1536]{1,0:T(8,128)(2,1)} %get-tuple-element.65.left, bf16[8,4,192,768]{3,2,1,0:T(8,128)(2,1)} %get-tuple-element.69.weight), custom_call_target="tpu_custom_call" | custom-call | flops 4831838208 | bytes 9437184 | tf_op jit(solution)/shard_map/pallas_call | solution.py:150
  218.5 9.8 %shard_map.289 = (bf16[512,3072]{1,0:T(8,128)(2,1)}, bf16[1536,512]{1,0:T(8,128)(2,1)}) custom-call(bf16[512,1536]{1,0:T(8,128)(2,1)} %cot.1, bf16[8,4,192,768]{3,2,1,0:T(8,128)(2,1)} %get-tuple-element.70.weight), custom_call_target="tpu_custom_call" | custom-call | flops 4831838208 | bytes 9437184 | tf_op jit(solution)/shard_map/pallas_call | solution.py:150
  228.2 22.4 %gate_norm.1 = (bf16[2,512,3072]{2,1,0:T(8,128)(2,1)}, bf16[512,3072]{1,0:T(8,128)(2,1)}, bf16[128,3072]{1,0:T(8,128)(2,1)}, f32[8,3072]{1,0:T(8,128)}) custom-call(bf16[512,3072]{1,0:T(8,128)(2,1)} %get-tuple-element.63.y, bf16[512,3072]{1,0:T(8,128)(2,1)} %get-tuple-element.64.signal, bf16[512,3072]{1,0:T(8,128)(2,1)} %shard_map.288.gate, ...), custom_call_target="tpu_custom_call" | custom-call | flops 10000000000 | bytes 25000000 | tf_op jit(solution)/shard_map/gate_norm/pallas_call | solution.py:419
  252.4 14.0 %collective-permute-start.3 = (bf16[144,3072]{1,0:T(8,128)(2,1)S(1)}, bf16[144,3072]{1,0:T(8,128)(2,1)S(1)}, u32[]{:S(2)}, u32[]{:S(2)}) collective-permute-start(bf16[144,3072]{1,0:T(8,128)(2,1)S(1)} %pad_maximum_fusion), channel_id=1, source_target_pairs={{1,0},{2,1},{3,2},{4,3},{5,4},{6,5},{7,6},{8,7},{9,8},{10,9},{11,1... | collective-permute-start | bytes 2654216 | tf_op jit(solution)/shard_map/ppermute | solution.py:1559
  268.4 17.2 %collective-permute-done.3 = bf16[144,3072]{1,0:T(8,128)(2,1)S(1)} collective-permute-done((bf16[144,3072]{1,0:T(8,128)(2,1)S(1)}, bf16[144,3072]{1,0:T(8,128)(2,1)S(1)}, u32[]{:S(2)}, u32[]{:S(2)}) %collective-permute-start.3) | collective-permute-done | bytes 884768 | tf_op jit(solution)/shard_map/ppermute | solution.py:1559
  288.1 4.6 collective-permute-start.4
  292.7 10.8 %out_project.1 = bf16[512,1536]{1,0:T(8,128)(2,1)} custom-call(bf16[2,512,3072]{2,1,0:T(8,128)(2,1)} %get-tuple-element.75.left.own, bf16[8,4,192,768]{3,2,1,0:T(8,128)(2,1)} %get-tuple-element.70.weight, bf16[512,1536]{1,0:T(8,128)(2,1)} %tokens.3), custom_call_target="tpu_custom_call" | custom-call | flops 4831838208 | bytes 9437184 | tf_op jit(solution)/shard_map/out_project/pallas_call | solution.py:740
  303.5 10.6 %gate_part.1.so_far = f32[512,1536]{1,0:T(8,128)} custom-call(bf16[2,512,3072]{2,1,0:T(8,128)(2,1)} %get-tuple-element.75.left.own, bf16[8,4,192,768]{3,2,1,0:T(8,128)(2,1)} %get-tuple-element.69.weight), custom_call_target="tpu_custom_call" | custom-call | flops 4831838208 | bytes 9437184 | tf_op jit(solution)/shard_map/gate_part/pallas_call | solution.py:775
  314.1 16.3 %collective-permute-done.4 = bf16[144,3072]{1,0:T(8,128)(2,1)S(1)} collective-permute-done((bf16[144,3072]{1,0:T(8,128)(2,1)S(1)}, bf16[144,3072]{1,0:T(8,128)(2,1)S(1)}, u32[]{:S(2)}, u32[]{:S(2)}) %collective-permute-start.4) | collective-permute-done | bytes 884768 | tf_op jit(solution)/shard_map/ppermute | solution.py:1559
  331.7 22.3 %shard_map.290 = (bf16[2,2,192,1536]{3,2,1,0:T(8,128)(2,1)}, bf16[2,2,192,1536]{3,2,1,0:T(8,128)(2,1)}, bf16[2,2,192,1536]{3,2,1,0:T(8,128)(2,1)}, bf16[2,2,192,1536]{3,2,1,0:T(8,128)(2,1)}) custom-call(s32[3]{0:T(128)} %pad_add_fusion.where, bf16[8,192,512]{2,1,0:T(8,128)(2,1)} %bitcast.29, bf16[8,192,512]{2,1,0:T(8,128)(2,1)} %bitcast.7.next_z.left_next, ...), custom_call_target="tpu_custom_call" | custom-call | flops 9663676416 | bytes 28311552 | tf_op jit(solution)/shard_map/pallas_call | solution.py:704
  354.0 3.1 collective-permute-start.9
  357.0 42.5 %ssd_backward.1 = (bf16[512,3072]{1,0:T(8,128)(2,1)}, f32[8,3072]{1,0:T(8,128)}, f32[8,3072]{1,0:T(8,128)}, f32[8,3072]{1,0:T(8,128)}, bf16[512,384]{1,0:T(8,128...) custom-call(bf16[528,3072]{1,0:T(8,128)(2,1)} %get-tuple-element.60.x, ...), custom_call_target="tpu_custom_call" | custom-call | flops 40000000000 | bytes 15000000 | tf_op jit(solution)/shard_map/ssd_backward/pallas_call | solution.py:591
  399.5 9.2 %collective-permute-done.9 = bf16[2,2,192,1536]{3,2,1,0:T(8,128)(2,1)} collective-permute-done((bf16[2,2,192,1536]{3,2,1,0:T(8,128)(2,1)}, bf16[2,2,192,1536]{3,2,1,0:T(8,128)(2,1)}, u32[]{:S(2)}, u32[]{:S(2)}) %collective-permute-start.9) | collective-permute-done | bytes 2359328 | tf_op jit(solution)/shard_map/ppermute | solution.py:1584
  408.7 3.8 add_convert_fusion.2
  412.6 3.7 add_convert_fusion
  416.2 116.8 %finish.1 = (f32[192,768]{1,0:T(8,128)}, f32[192,64]{1,0:T(8,128)}, f32[192,12]{1,0:T(8,128)}, f32[192,768]{1,0:T(8,128)}, f32[768,192]{1,0:T(8,128)}, /*index=5...) custom-call(bf16[512,3072]{1,0:T(8,128)(2,1)} %get-tuple-element.78.dx, ...), custom_call_target="tpu_custom_call" | custom-call | flops 60000002048 | bytes 1000000 | tf_op jit(solution)/shard_map/finish/pallas_call | solution.py:1524
  533.1 1.5 slice.117
  534.6 1.7 fusion.6
  539.5 1.6 copy.35
  541.1 1.6 copy.36
  543.4 2.2 copy.37
  546.8 3.9 copy.41
  (79 shorter events, 31.3 us)
Async XLA Ops:
  2.9 92.0 %collective-permute-start = (bf16[32,1536]{1,0:T(8,128)(2,1)}, bf16[32,1536]{1,0:T(8,128)(2,1)}, u32[]{:S(2)}, u32[]{:S(2)}) collective-permute-start(bf16[32,1536]{1,0:T(8,128)(2,1)} %fusion.1), channel_id=1, source_target_pairs={{0,1},{1,2},{2,3},{3,4},{4,5},{5,6},{6,7},{7,8},{8,9},{9,10},{10,1... | collective-permute-start | bytes 294920 | tf_op jit(solution)/shard_map/ppermute | solution.py:1559
  9.2 1.0 copy-start.1
  10.1 1.0 copy-start.2
  11.1 73.0 %copy-start.12 = (bf16[1536]{0:T(1024)(128)(2,1)S(1)}, bf16[1536]{0:T(1024)(128)(2,1)}, u32[]{:S(2)}) copy-start(bf16[1536]{0:T(1024)(128)(2,1)} %param.20) | copy-start | bytes 9220
  11.1 73.6 %copy-start.10 = (bf16[3072]{0:T(1024)(128)(2,1)S(1)}, bf16[3072]{0:T(1024)(128)(2,1)}, u32[]{:S(2)}) copy-start(bf16[3072]{0:T(1024)(128)(2,1)} %param.26) | copy-start | bytes 18436
  11.1 73.7 %copy-start.13 = (bf16[48]{0:T(256)(128)(2,1)S(1)}, bf16[48]{0:T(256)(128)(2,1)}, u32[]{:S(2)}) copy-start(bf16[48]{0:T(256)(128)(2,1)} %param.31) | copy-start | bytes 292
  77.8 4.2 copy-start.3
  82.0 46.5 %collective-permute-start.1 = (bf16[4,192,768]{2,1,0:T(8,128)(2,1)S(1)}, bf16[4,192,768]{2,1,0:T(8,128)(2,1)S(1)}, u32[]{:S(2)}, u32[]{:S(2)}) collective-permute-start(bf16[4,192,768]{2,1,0:T(8,128)(2,1)S(1)} %get-tuple-element.67.z_line), channel_id=1, source_target_pairs={{0,8},{4,12},{8,0},{12,4},{16,24},{20,28},{24,16},{28,20},{1,9},{5... | collective-permute-start | bytes 3538952 | tf_op jit(solution)/shard_map/ppermute | solution.py:1584
  84.0 44.4 %collective-permute-start.2 = (bf16[4,192,768]{2,1,0:T(8,128)(2,1)S(1)}, bf16[4,192,768]{2,1,0:T(8,128)(2,1)}, u32[]{:S(2)}, u32[]{:S(2)}) collective-permute-start(bf16[4,192,768]{2,1,0:T(8,128)(2,1)S(1)} %get-tuple-element.68.o_line), channel_id=1, source_target_pairs={{0,16},{4,20},{8,24},{12,28},{16,0},{20,4},{24,8},{28,12},{1,17},{... | collective-permute-start | bytes 3538952 | tf_op jit(solution)/shard_map/ppermute | solution.py:1584
  128.4 1.2 copy-start
  208.2 0.9 copy-start.4
  250.6 35.8 %copy-start.5 = (bf16[128,3072]{1,0:T(8,128)(2,1)S(1)}, bf16[128,3072]{1,0:T(8,128)(2,1)}, u32[]{:S(2)}) copy-start(bf16[128,3072]{1,0:T(8,128)(2,1)} %get-tuple-element.77) | copy-start | bytes 2359300
  250.7 81.0 %collective-permute-start.8 = (bf16[2,512,3072]{2,1,0:T(8,128)(2,1)}, bf16[2,512,3072]{2,1,0:T(8,128)(2,1)}, u32[]{:S(2)}, u32[]{:S(2)}) collective-permute-start(bf16[2,512,3072]{2,1,0:T(8,128)(2,1)} %get-tuple-element.75.left.own), channel_id=1, source_target_pairs={{0,4},{4,0},{8,12},{12,8},{16,20},{20,16},{24,28},{28,24},{1,5},{5... | collective-permute-start | bytes 18874376 | tf_op jit(solution)/shard_map/ppermute | solution.py:1584
  252.4 33.2 %collective-permute-start.3 = (bf16[144,3072]{1,0:T(8,128)(2,1)S(1)}, bf16[144,3072]{1,0:T(8,128)(2,1)S(1)}, u32[]{:S(2)}, u32[]{:S(2)}) collective-permute-start(bf16[144,3072]{1,0:T(8,128)(2,1)S(1)} %pad_maximum_fusion), channel_id=1, source_target_pairs={{1,0},{2,1},{3,2},{4,3},{5,4},{6,5},{7,6},{8,7},{9,8},{10,9},{11,1... | collective-permute-start | bytes 2654216 | tf_op jit(solution)/shard_map/ppermute | solution.py:1559
  267.0 64.6 %collective-permute-start.6 = (bf16[1536,512]{1,0:T(8,128)(2,1)}, bf16[1536,512]{1,0:T(8,128)(2,1)}, u32[]{:S(2)}, u32[]{:S(2)}) collective-permute-start(bf16[1536,512]{1,0:T(8,128)(2,1)} %get-tuple-element.84), channel_id=1, source_target_pairs={{0,4},{4,0},{8,12},{12,8},{16,20},{20,16},{24,28},{28,24},{1,5},{5... | collective-permute-start | bytes 4718600 | tf_op jit(solution)/shard_map/ppermute | solution.py:1584
  267.9 63.8 %collective-permute-start.7 = (bf16[1536,512]{1,0:T(8,128)(2,1)}, bf16[1536,512]{1,0:T(8,128)(2,1)}, u32[]{:S(2)}, u32[]{:S(2)}) collective-permute-start(bf16[1536,512]{1,0:T(8,128)(2,1)} %get-tuple-element.85), channel_id=1, source_target_pairs={{0,4},{4,0},{8,12},{12,8},{16,20},{20,16},{24,28},{28,24},{1,5},{5... | collective-permute-start | bytes 4718600 | tf_op jit(solution)/shard_map/ppermute | solution.py:1584
  286.8 27.2 %collective-permute-start.5 = (bf16[144,3072]{1,0:T(8,128)(2,1)S(1)}, bf16[144,3072]{1,0:T(8,128)(2,1)S(1)}, u32[]{:S(2)}, u32[]{:S(2)}) collective-permute-start(bf16[144,3072]{1,0:T(8,128)(2,1)S(1)} %pad_maximum_fusion.1), channel_id=1, source_target_pairs={{3,0},{4,1},{5,2},{6,3},{7,4},{8,5},{9,6},{10,7},{11,8},{12,9},{13... | collective-permute-start | bytes 2654216 | tf_op jit(solution)/shard_map/ppermute | solution.py:1559
  288.1 42.3 %collective-permute-start.4 = (bf16[144,3072]{1,0:T(8,128)(2,1)S(1)}, bf16[144,3072]{1,0:T(8,128)(2,1)S(1)}, u32[]{:S(2)}, u32[]{:S(2)}) collective-permute-start(bf16[144,3072]{1,0:T(8,128)(2,1)S(1)} %pad_maximum_fusion.1), channel_id=1, source_target_pairs={{1,0},{2,1},{3,2},{4,3},{5,4},{6,5},{7,6},{8,7},{9,8},{10,9},{11,1... | collective-permute-start | bytes 2654216 | tf_op jit(solution)/shard_map/ppermute | solution.py:1559
  354.0 54.8 %collective-permute-start.9 = (bf16[2,2,192,1536]{3,2,1,0:T(8,128)(2,1)}, bf16[2,2,192,1536]{3,2,1,0:T(8,128)(2,1)}, u32[]{:S(2)}, u32[]{:S(2)}) collective-permute-start(bf16[2,2,192,1536]{3,2,1,0:T(8,128)(2,1)} %get-tuple-element.87), channel_id=1, source_target_pairs={{0,8},{4,12},{8,0},{12,4},{16,24},{20,28},{24,16},{28,20},{1,9},{5... | collective-permute-start | bytes 7077896 | tf_op jit(solution)/shard_map/ppermute | solution.py:1584
  357.0 55.6 %collective-permute-start.10 = (bf16[2,2,192,1536]{3,2,1,0:T(8,128)(2,1)}, bf16[2,2,192,1536]{3,2,1,0:T(8,128)(2,1)}, u32[]{:S(2)}, u32[]{:S(2)}) collective-permute-start(bf16[2,2,192,1536]{3,2,1,0:T(8,128)(2,1)} %get-tuple-element.89), channel_id=1, source_target_pairs={{0,16},{4,20},{8,24},{12,28},{16,0},{20,4},{24,8},{28,12},{1,17},{... | collective-permute-start | bytes 7077896 | tf_op jit(solution)/shard_map/ppermute | solution.py:1584
  357.0 51.7 %copy-start.7 = (bf16[2,2,192,1536]{3,2,1,0:T(8,128)(2,1)S(1)}, bf16[2,2,192,1536]{3,2,1,0:T(8,128)(2,1)}, u32[]{:S(2)}) copy-start(bf16[2,2,192,1536]{3,2,1,0:T(8,128)(2,1)} %get-tuple-element.86) | copy-start | bytes 7077892
  408.7 3.8 copy-start.6
  533.1 12.5 %copy-start.11 = (f32[1,1536]{1,0:T(1,128)S(1)}, f32[1,1536]{1,0:T(1,128)}, u32[]{:S(2)}) copy-start(f32[1,1536]{1,0:T(1,128)} %get-tuple-element.95) | copy-start | bytes 18436
  546.8 3.9 copy-start.9
  546.8 4.7 copy-start.8
